TPU v7x, 16 devices: a whole 2x2x2 slice. The times are simulated.
16 devices in a mesh: ep: 16 (over z, y, x, core).
Axes of the slice: x: 2, y: 2, z: 2, core: 2. Of those that a mesh axis runs over, the one named last changes fastest.
Arguments:
- tokens: bfloat16 [2048, 4096], P('ep')
- k_cache: bfloat16 [2048, 128, 8, 128], P('ep')
- v_cache: bfloat16 [2048, 128, 8, 128], P('ep')
- positions: int32 [2048], P('ep')
- expert_one: int32 [2048], P('ep')
- expert_two: int32 [2048], P('ep')
- eligible: int32 [2048, 16], P('ep')
- ln1_gain: bfloat16 [4096], replicated
- ln1_bias: bfloat16 [4096], replicated
- w_query: bfloat16 [4096, 4096], replicated
- b_query: bfloat16 [4096], replicated
- w_key: bfloat16 [4096, 1024], replicated
- b_key: bfloat16 [1024], replicated
- w_value: bfloat16 [4096, 1024], replicated
- b_value: bfloat16 [1024], replicated
- w_out: bfloat16 [4096, 4096], replicated
- b_out: bfloat16 [4096], replicated
- ln2_gain: bfloat16 [4096], replicated
- ln2_bias: bfloat16 [4096], replicated
- w_router: bfloat16 [4096, 16], replicated
- w_gate: bfloat16 [16, 4096, 960], P('ep')
- w_up: bfloat16 [16, 4096, 960], P('ep')
- w_down: bfloat16 [16, 960, 4096], P('ep')
Outputs:
- output 1: bfloat16 [2048, 4096], P('ep')
- output 2: bfloat16 [2048, 8, 128], P('ep')
- output 3: bfloat16 [2048, 8, 128], P('ep')
All inputs are finite; a program needn't handle non-finite values.
Results may differ from a plain program's by a relative error of at most 0.00965712.
Values are sent between devices in bfloat16 or wider.
A program may use at most 1 GiB of HBM per device.

v0:
```python
import jax
import jax.numpy as jnp
from jax import lax
from jax.sharding import PartitionSpec as P

ROPE_BASE = 10000.0
LN_EPS = 1e-5


def layer_norm(values_in, gain, bias):
    mean_val = jnp.mean(values_in, axis=-1, keepdims=True)
    centered = values_in - mean_val
    var_val = jnp.mean(centered * centered, axis=-1, keepdims=True)
    return centered * lax.rsqrt(var_val + LN_EPS) * gain.astype(jnp.float32) + bias.astype(jnp.float32)


def rope_tables(positions, head_dim):
    half_dim = head_dim // 2
    inv_freq = ROPE_BASE ** (jnp.arange(half_dim, dtype=jnp.float32) * (-2.0 / head_dim))
    angles = positions.astype(jnp.float32)[:, None] * inv_freq[None, :]
    angles = jnp.concatenate([angles, angles], axis=-1)
    return jnp.cos(angles), jnp.sin(angles)


def apply_rope(values_in, cos_tab, sin_tab):
    half_dim = values_in.shape[-1] // 2
    rotated = jnp.concatenate([-values_in[..., half_dim:], values_in[..., :half_dim]], axis=-1)
    return values_in * cos_tab[:, None, :] + rotated * sin_tab[:, None, :]


def attention_block(tokens, k_cache, v_cache, positions, ln1_gain, ln1_bias, w_query, b_query, w_key, b_key, w_value, b_value, w_out, b_out):
    tok_count, seq_len, kv_heads, head_dim = k_cache.shape
    num_heads = w_query.shape[1] // head_dim
    group_size = num_heads // kv_heads
    x_f = tokens.astype(jnp.float32)
    h_one = layer_norm(x_f, ln1_gain, ln1_bias).astype(jnp.bfloat16)
    cos_tab, sin_tab = rope_tables(positions, head_dim)
    q_lin = jnp.dot(h_one, w_query, preferred_element_type=jnp.float32) + b_query.astype(jnp.float32)
    q_rot = apply_rope(q_lin.reshape(tok_count, num_heads, head_dim), cos_tab, sin_tab).astype(jnp.bfloat16)
    q_grp = q_rot.reshape(tok_count, kv_heads, group_size, head_dim)
    k_lin = jnp.dot(h_one, w_key, preferred_element_type=jnp.float32) + b_key.astype(jnp.float32)
    key_new = apply_rope(k_lin.reshape(tok_count, kv_heads, head_dim), cos_tab, sin_tab).astype(jnp.bfloat16)
    v_lin = jnp.dot(h_one, w_value, preferred_element_type=jnp.float32) + b_value.astype(jnp.float32)
    value_new = v_lin.astype(jnp.bfloat16).reshape(tok_count, kv_heads, head_dim)
    score_scale = head_dim ** -0.5
    s_cache = jnp.einsum('tkgd,tskd->tkgs', q_grp, k_cache, preferred_element_type=jnp.float32) * score_scale
    valid_mask = jnp.arange(seq_len)[None, None, None, :] < positions[:, None, None, None]
    s_cache = jnp.where(valid_mask, s_cache, -jnp.inf)
    s_new = jnp.einsum('tkgd,tkd->tkg', q_grp, key_new, preferred_element_type=jnp.float32) * score_scale
    top_val = jnp.maximum(jnp.max(s_cache, axis=-1), s_new)
    e_cache = jnp.exp(s_cache - top_val[..., None])
    e_new = jnp.exp(s_new - top_val)
    denom_sum = jnp.sum(e_cache, axis=-1) + e_new
    p_cache = (e_cache / denom_sum[..., None]).astype(jnp.bfloat16)
    p_new = (e_new / denom_sum).astype(jnp.bfloat16)
    attn_vals = jnp.einsum('tkgs,tskd->tkgd', p_cache, v_cache, preferred_element_type=jnp.float32)
    attn_vals = attn_vals + p_new.astype(jnp.float32)[..., None] * value_new.astype(jnp.float32)[:, :, None, :]
    attn_flat = attn_vals.astype(jnp.bfloat16).reshape(tok_count, num_heads * head_dim)
    x_mid = (x_f + jnp.dot(attn_flat, w_out, preferred_element_type=jnp.float32) + b_out.astype(jnp.float32)).astype(jnp.bfloat16)
    return x_mid, key_new, value_new


def router_gates(h_two, w_router, expert_one, expert_two, eligible):
    logits = jnp.dot(h_two, w_router, preferred_element_type=jnp.float32)
    expert_ids = jnp.arange(logits.shape[1])[None, :]
    hit_one = expert_ids == expert_one[:, None]
    hit_two = expert_ids == expert_two[:, None]
    keep_one = eligible == 1
    keep_two = keep_one & jnp.logical_not(hit_one)
    prob_one = jax.nn.softmax(jnp.where(keep_one, logits, -jnp.inf), axis=-1)
    prob_two = jax.nn.softmax(jnp.where(keep_two, logits, -jnp.inf), axis=-1)
    gate_one = jnp.sum(jnp.where(hit_one, prob_one, 0.0), axis=-1)
    gate_two = jnp.sum(jnp.where(hit_two, prob_two, 0.0), axis=-1)
    return gate_one, gate_two


def send_plan(expert_one, expert_two, local_experts, groups, tok_count):
    num_experts = local_experts * groups
    pair_expert = jnp.concatenate([expert_one, expert_two])
    token_ids = jnp.arange(tok_count, dtype=jnp.int32)
    pair_token = jnp.concatenate([token_ids, token_ids])
    one_hot = (pair_expert[:, None] == jnp.arange(num_experts, dtype=jnp.int32)[None, :]).astype(jnp.int32)
    pair_slot = jnp.sum(one_hot * jnp.cumsum(one_hot, axis=0), axis=1) - 1
    buffer_row = ((pair_expert % local_experts) * groups + pair_expert // local_experts) * tok_count + pair_slot
    src_token = jax.ops.segment_sum(pair_token, buffer_row, num_segments=num_experts * tok_count)
    return buffer_row, src_token


def expert_mlp(expert_in, w_gate, w_up, w_down):
    u_val = jnp.einsum('emd,edf->emf', expert_in, w_gate, preferred_element_type=jnp.float32)
    v_val = jnp.einsum('emd,edf->emf', expert_in, w_up, preferred_element_type=jnp.float32)
    z_val = (jax.nn.silu(u_val) * v_val).astype(jnp.bfloat16)
    return jnp.einsum('emf,efd->emd', z_val, w_down, preferred_element_type=jnp.float32).astype(jnp.bfloat16)


def solution(mesh):
    groups = mesh.shape['ep']

    def local_step(tokens, k_cache, v_cache, positions, expert_one, expert_two, eligible, ln1_gain, ln1_bias, w_query, b_query, w_key, b_key, w_value, b_value, w_out, b_out, ln2_gain, ln2_bias, w_router, w_gate, w_up, w_down):
        x_mid, key_new, value_new = attention_block(tokens, k_cache, v_cache, positions, ln1_gain, ln1_bias, w_query, b_query, w_key, b_key, w_value, b_value, w_out, b_out)
        h_two = layer_norm(x_mid.astype(jnp.float32), ln2_gain, ln2_bias).astype(jnp.bfloat16)
        gate_one, gate_two = router_gates(h_two, w_router, expert_one, expert_two, eligible)
        tok_count, d_model = h_two.shape
        local_experts = w_gate.shape[0]
        num_experts = local_experts * groups
        buffer_row, src_token = send_plan(expert_one, expert_two, local_experts, groups, tok_count)
        send_rows = jnp.take(h_two, src_token, axis=0).reshape(local_experts, groups, tok_count, d_model)
        recv_rows = lax.all_to_all(send_rows, 'ep', 1, 1, tiled=True)
        expert_in = recv_rows.reshape(local_experts, groups * tok_count, d_model)
        expert_out = expert_mlp(expert_in, w_gate, w_up, w_down)
        back_rows = lax.all_to_all(expert_out.reshape(local_experts, groups, tok_count, d_model), 'ep', 1, 1, tiled=True)
        back_flat = back_rows.reshape(num_experts * tok_count, d_model)
        out_one = jnp.take(back_flat, buffer_row[:tok_count], axis=0)
        out_two = jnp.take(back_flat, buffer_row[tok_count:], axis=0)
        y_sum = gate_one[:, None] * out_one.astype(jnp.float32) + gate_two[:, None] * out_two.astype(jnp.float32)
        tokens_out = (x_mid.astype(jnp.float32) + y_sum).astype(jnp.bfloat16)
        return tokens_out, key_new, value_new

    row_spec = P('ep', None)
    cache_spec = P('ep', None, None, None)
    vec_spec = P('ep')
    rep_one = P(None)
    rep_two = P(None, None)
    expert_spec = P('ep', None, None)
    in_specs = (row_spec, cache_spec, cache_spec, vec_spec, vec_spec, vec_spec, row_spec, rep_one, rep_one, rep_two, rep_one, rep_two, rep_one, rep_two, rep_one, rep_two, rep_one, rep_one, rep_one, rep_two, expert_spec, expert_spec, expert_spec)
    out_specs = (row_spec, expert_spec, expert_spec)
    return jax.shard_map(local_step, mesh=mesh, in_specs=in_specs, out_specs=out_specs, check_vma=False)
```

profile of v0, /device:TPU:0, one launch (start us, length us, event | category | flops | bytes accessed | tf_op | source)
XLA Modules:
  0.0 635.4 jit_solution(13230268141888745797)
XLA Ops:
  0.7 0.7 convert_element_type.99
  1.5 0.7 iota_compare_fusion
  2.2 0.7 constant_dynamic-update-slice_fusion.1
  2.9 0.7 constant_dynamic-update-slice_fusion
  3.5 0.6 reduce-window.6
  4.5 0.6 multiply_add_fusion
  5.0 0.7 fusion.56
  5.7 2.1 scatter_custom_fusion
  7.9 1.5 convert_reduce_fusion
  9.3 1.7 fusion.16
  11.1 13.0 %convolution_add_fusion.1 = f32[128,4096]{1,0:T(8,128)S(1)} fusion(bf16[4096,4096]{1,0:T(8,128)(2,1)} %param.34, f32[4096]{0:T(1024)S(1)} %convert_element_type.98, bf16[128,4096]{1,0:T(8,128)(2,1)S(1)} %copy-done.3, f32[4096]{0:T(1024)S(1)} %convert_element_type.96, f32[4096]{0:T(1024)S(1)} %convert_element_type.95, f32[128]{0:T(128)S(1)} %add_rsqrt_fusion.1, ...), kind=kOutput, calls=%fused_computation.18 | convolution fusion | flops 4298637312 | bytes 36750336 | tf_op jit(solution)/shard_map/dot_general | solution.py:38
  24.1 2.5 reshape.271
  26.6 0.4 copy.57
  26.9 0.7 slice_negate_fusion
  27.8 0.3 fusion.39
  28.1 4.7 fusion.25
  33.4 1.2 copy-done.4
  34.6 1.7 fusion.21
  36.3 1.0 copy-done.6
  37.2 1.2 fusion.36
  38.7 23.5 %fusion.22 = (f32[128,8,4]{2,1,0:T(8,128)}, f32[128,8,4,128]{3,2,1,0:T(4,128)S(1)}) fusion(pred[128,128]{1,0:T(8,128)(4,1)S(1)} %iota_compare_fusion, bf16[128,8,4,128]{3,2,1,0:T(4,128)(2,1)} %copy-done.6, bf16[128,128,8,128]{3,2,1,0:T(8,128)(2,1)} %param.26), kind=kOutput, calls=%fused_computation.40 | convolution fusion | flops 135786496 | bytes 36732928 | tf_op jit(solution)/shard_map/tkgd,tskd->tkgs/dot_general | solution.py:46
  62.1 1.2 copy.45
  63.4 1.0 copy.46
  64.4 4.4 fusion.28
  68.8 1.2 copy.47
  70.1 1.0 copy.48
  71.1 1.0 copy.50
  72.2 4.8 fusion.27
  77.1 0.6 copy-done.7
  77.8 17.4 %add_convert_fusion.2 = bf16[128,8,4,128]{3,2,1,0:T(4,128)(2,1)} fusion(bf16[128,128,8,128]{3,2,1,0:T(8,128)(2,1)} %param.27, f32[128,8,4,128]{3,2,1,0:T(4,128)S(1)} %get-tuple-element.27, f32[128,8,128]{2,1,0:T(8,128)S(1)} %bitcast_convert_fusion, f32[128,8,4]{2,1,0:T(8,128)S(1)} %copy-done.9, f32[128,8,4]{2,1,0:T(8,128)S(1)} %copy-done.8, ...), kind=kOutput, calls=%fused_computation.36 | convolution fusion | flops 138412032 | bytes 37289984 | tf_op jit(solution)/shard_map/tkgs,tskd->tkgd/dot_general | solution.py:56
  95.2 1.8 reshape.275
  97.1 22.9 %fusion.62 = (f32[128]{0:T(128)S(1)}, f32[128,4096]{1,0:T(8,128)S(1)}) fusion(f32[4096]{0:T(1024)S(1)} %convert_element_type.110, bf16[128,4096]{1,0:T(8,128)(2,1)S(1)} %reshape.275, bf16[4096,4096]{1,0:T(8,128)(2,1)} %param.40, bf16[128,4096]{1,0:T(8,128)(2,1)S(1)} %copy-done.3), kind=kOutput, calls=%fused_computation.117 | convolution fusion | flops 4298113024 | bytes 37765632 | tf_op jit(solution)/shard_map/dot_general | solution.py:59
  120.0 0.4 multiply_reduce_fusion
  120.4 0.3 copy-done.16
  120.8 0.5 copy-done.1
  121.3 0.4 add_convert_fusion.1
  121.7 14.3 %gather_fusion = bf16[2048,4096]{1,0:T(8,128)(2,1)} fusion(bf16[128,4096]{1,0:T(8,128)(2,1)S(1)} %add_convert_fusion.1, s32[2048]{0:T(1024)S(1)} %fusion.50), kind=kCustom, calls=%fused_computation.2 | custom fusion | bytes 33562624 | tf_op jit(solution)/shard_map/jit(_take)/gather | solution.py:107
  136.0 8.5 %broadcast_select_fusion = bf16[1,16,128,4096]{3,2,0,1:T(8,128)(2,1)S(1)} fusion(bf16[1,16,128,4096]{3,2,0,1:T(8,128)(2,1)} %bitcast.82, pred[16,128]{1,0:T(8,128)(4,1)S(1)} %and_bitcast_fusion), kind=kLoop, calls=%fused_computation.8 | loop fusion | flops 8388608 | bytes 33556480 | tf_op jit(solution)/shard_map/jit(_take)/select_n | solution.py:107
  144.5 192.0 %all_to_all.10 = bf16[1,16,128,4096]{3,2,0,1:T(8,128)(2,1)S(1)} all-to-all(bf16[1,16,128,4096]{3,2,0,1:T(8,128)(2,1)S(1)} %broadcast_select_fusion), channel_id=1, replica_groups=mesh['ep'=16] {'ep'}, dimensions={1} | all-to-all | bytes 33554432 | tf_op jit(solution)/shard_map/all_to_all | solution.py:108
  336.5 20.3 %fusion.5 = f32[2048,960]{0,1:T(8,128)} fusion(bf16[2048,4096]{1,0:T(8,128)(2,1)S(1)} %bitcast.86, bf16[1,4096,960]{1,2,0:T(8,128)(2,1)} %param.46), kind=kOutput, calls=%fused_computation.11 | convolution fusion | flops 16106127360 | bytes 32505856 | tf_op jit(solution)/shard_map/emd,edf->emf/dot_general | solution.py:91
  356.8 20.5 %multiply_convert_fusion = bf16[2048,960]{0,1:T(8,128)(2,1)S(1)} fusion(f32[2048,960]{0,1:T(8,128)} %fusion.5, bf16[2048,4096]{1,0:T(8,128)(2,1)S(1)} %bitcast.87, bf16[1,4096,960]{1,2,0:T(8,128)(2,1)} %param.45), kind=kOutput, calls=%fused_computation.15 | convolution fusion | flops 16117923840 | bytes 36438016 | tf_op jit(solution)/shard_map/emd,edf->emf/dot_general | solution.py:90
  377.3 23.9 %convolution_convert_fusion = bf16[2048,4096]{1,0:T(8,128)(2,1)} fusion(bf16[2048,960]{0,1:T(8,128)(2,1)S(1)} %multiply_convert_fusion, bf16[1,960,4096]{2,1,0:T(8,128)(2,1)} %param.47), kind=kOutput, calls=%fused_computation.9 | convolution fusion | flops 16114515968 | bytes 28573696 | tf_op jit(solution)/shard_map/emf,efd->emd/dot_general | solution.py:93
  401.2 4.0 all-to-all-start.1
  405.3 0.4 fusion.54
  405.8 204.8 %all-to-all-done.1 = bf16[1,16,128,4096]{3,2,0,1:T(8,128)(2,1)} async-done(((bf16[1,16,128,4096]{3,2,0,1:T(8,128)(2,1)}), bf16[1,16,128,4096]{3,2,0,1:T(8,128)(2,1)}, u32[]{:S(2)}, u32[]{:S(2)}) %all-to-all-start.1) | async-done | bytes 16777248 | tf_op jit(solution)/shard_map/all_to_all | solution.py:111
  610.6 10.1 %gather_fusion.1 = bf16[128,4096]{1,0:T(8,128)(2,1)S(1)} fusion(bf16[2048,4096]{1,0:T(8,128)(2,1)} %bitcast.19, s32[1024]{0:T(1024)S(1)} %get-tuple-element.32), kind=kCustom, calls=%fused_computation.clone | custom fusion | bytes 2097664 | tf_op jit(solution)/shard_map/jit(_take)/gather | solution.py:113
  620.7 11.2 %gather_fusion.2 = bf16[128,4096]{1,0:T(8,128)(2,1)} fusion(bf16[2048,4096]{1,0:T(8,128)(2,1)} %bitcast.19, s32[1024]{0:T(1024)S(1)} %get-tuple-element.31), kind=kCustom, calls=%fused_computation.1.clone | custom fusion | bytes 2097664 | tf_op jit(solution)/shard_map/jit(_take)/gather | solution.py:114
  632.0 3.0 add_convert_fusion
  (78 shorter events, 1.6 us)
Async XLA Ops:
  0.6 404.7 %copy-start = (bf16[4096,16]{0,1:T(8,128)(2,1)S(1)}, bf16[4096,16]{0,1:T(8,128)(2,1)}, u32[]{:S(2)}) copy-start(bf16[4096,16]{0,1:T(8,128)(2,1)} %param.44) | copy-start | bytes 393220
  0.6 10.4 %copy-start.3 = (bf16[128,4096]{1,0:T(8,128)(2,1)S(1)}, bf16[128,4096]{1,0:T(8,128)(2,1)}, u32[]{:S(2)}) copy-start(bf16[128,4096]{1,0:T(8,128)(2,1)} %param.25) | copy-start | bytes 3145732
  0.7 10.3 %copy-start.12 = (bf16[4096]{0:T(1024)(128)(2,1)S(1)}, bf16[4096]{0:T(1024)(128)(2,1)}, u32[]{:S(2)}) copy-start(bf16[4096]{0:T(1024)(128)(2,1)} %param.32) | copy-start | bytes 24580
  0.7 10.3 %copy-start.13 = (bf16[4096]{0:T(1024)(128)(2,1)S(1)}, bf16[4096]{0:T(1024)(128)(2,1)}, u32[]{:S(2)}) copy-start(bf16[4096]{0:T(1024)(128)(2,1)} %param.33) | copy-start | bytes 24580
  0.7 10.4 %copy-start.14 = (bf16[4096]{0:T(1024)(128)(2,1)S(1)}, bf16[4096]{0:T(1024)(128)(2,1)}, u32[]{:S(2)}) copy-start(bf16[4096]{0:T(1024)(128)(2,1)} %param.35) | copy-start | bytes 24580
  26.9 1.1 copy-start.20
  32.9 1.7 copy-start.4
  33.4 2.9 copy-start.10
  36.3 1.0 copy-start.6
  64.4 7.7 %copy-start.21 = (bf16[1024]{0:T(1024)(128)(2,1)S(1)}, bf16[1024]{0:T(1024)(128)(2,1)}, u32[]{:S(2)}) copy-start(bf16[1024]{0:T(1024)(128)(2,1)} %param.39) | copy-start | bytes 6148
  72.2 5.6 copy-start.5
  72.2 5.6 copy-start.8
  72.2 5.6 copy-start.9
  77.1 0.7 copy-start.7
  95.2 1.9 copy-start.15
  120.0 1.3 copy-start.1
  120.0 0.7 copy-start.16
  120.0 0.8 copy-start.17
  401.2 4.1 copy-start.19
  401.2 4.1 copy-start.11
  401.2 4.5 copy-start.18
  401.2 4.6 copy-start.22
  401.2 209.4 %all-to-all-start.1 = ((bf16[1,16,128,4096]{3,2,0,1:T(8,128)(2,1)}), bf16[1,16,128,4096]{3,2,0,1:T(8,128)(2,1)}, u32[]{:S(2)}, u32[]{:S(2)}) async-start(bf16[1,16,128,4096]{3,2,0,1:T(8,128)(2,1)} %bitcast.85), calls=%async_computation.1 | async-start | bytes 33554432 | tf_op jit(solution)/shard_map/all_to_all | solution.py:111
  620.7 11.3 %copy-start.2 = (f32[128,4096]{1,0:T(8,128)S(1)}, f32[128,4096]{1,0:T(8,128)}, u32[]{:S(2)}) copy-start(f32[128,4096]{1,0:T(8,128)} %copy-done.1) | copy-start | bytes 6291460
where the time goes:
time: 644 us; the launch traced here: 635 us
  waiting for transfers between devices  205 us (32%)
  blocking collectives  192 us (30%)
  matrix products  153 us (24%)
  local copies, waits for them, and re-layouts  51.6 us (8%)
  other arithmetic  28.9 us (4%)
    all_to_all x1, waiting for transfers between devices, local_step(): lax.all_to_all(expert_out.reshape(local_experts, groups, tok_count, d_mod...  205 us
    all_to_all x1, blocking collectives, local_step(): recv_rows = lax.all_to_all(send_rows, 'ep', 1, 1, tiled=True)  192 us
    dot_general x1, matrix products, expert_mlp(): jnp.einsum('emf,efd->emd', z_val, w_down, preferred_element_type=jnp.floa...  23.9 us
    dot_general x1, matrix products, attention_block(): jnp.einsum('tkgd,tskd->tkgs', q_grp, k_cache, preferred_element_type=jnp....  23.5 us
    dot_general x1, matrix products, attention_block(): jnp.dot(attn_flat, w_out, preferred_element_type=jnp.float32)  22.9 us
    dot_general x1, matrix products, expert_mlp(): jnp.einsum('emd,edf->emf', expert_in, w_gate, preferred_element_type=jnp....  20.5 us
    dot_general x1, matrix products, expert_mlp(): jnp.einsum('emd,edf->emf', expert_in, w_up, preferred_element_type=jnp.fl...  20.3 us
    dot_general x1, matrix products, attention_block(): jnp.einsum('tkgs,tskd->tkgd', p_cache, v_cache, preferred_element_type=jn...  17.4 us
  transfers between devices with their start and end apart: 1, of which 1 were waited for; matrix products, arithmetic and copies ran while one was open for 0% of the time, Pallas kernels for 0%

commit v1 on v0

v1 whole, which is shorter than its diff:
```python
import functools

import jax
import jax.numpy as jnp
from jax import lax
from jax.experimental import pallas as pl
from jax.experimental.pallas import tpu as pltpu
from jax.sharding import PartitionSpec as P

ROPE_BASE = 10000.0
LN_EPS = 1e-5
CHUNKS = 2
MIB = 1024 * 1024


def layer_norm_rows(x, gain, bias):
    mean_val = jnp.mean(x, axis=-1, keepdims=True)
    centered = x - mean_val
    var_val = jnp.mean(centered * centered, axis=-1, keepdims=True)
    return centered * lax.rsqrt(var_val + LN_EPS) * gain + bias


def rope_tables(positions, head_dim):
    half_dim = head_dim // 2
    inv_freq = ROPE_BASE ** (jnp.arange(half_dim, dtype=jnp.float32) * (-2.0 / head_dim))
    angles = positions.astype(jnp.float32)[:, None] * inv_freq[None, :]
    cos_val, sin_val = jnp.cos(angles), jnp.sin(angles)
    return jnp.concatenate([cos_val, cos_val], axis=-1), jnp.concatenate([-sin_val, sin_val], axis=-1)


def qkv_kernel(head_dim, q_steps, kv_steps, tok_ref, gain_ref, bias_ref, cos_ref, sin_ref, wq_ref, wk_ref, wv_ref, bq_ref, bk_ref, bv_ref, q_ref, k_ref, v_ref, h_ref):
    step = pl.program_id(0)

    @pl.when(step == 0)
    def _():
        x = tok_ref[...].astype(jnp.float32)
        h_ref[...] = layer_norm_rows(x, gain_ref[...].astype(jnp.float32), bias_ref[...].astype(jnp.float32)).astype(jnp.bfloat16)

    def project(w_ref, b_ref):
        return jnp.dot(h_ref[...], w_ref[...], preferred_element_type=jnp.float32) + b_ref[...].astype(jnp.float32)

    def rotated(y, out_ref):
        for head in range(y.shape[1] // head_dim):
            cols = slice(head * head_dim, (head + 1) * head_dim)
            part = y[:, cols]
            turned = pltpu.roll(part, head_dim // 2, 1)
            out_ref[:, cols] = (part * cos_ref[...] + turned * sin_ref[...]).astype(jnp.bfloat16)

    @pl.when(step < q_steps)
    def _():
        rotated(project(wq_ref, bq_ref), q_ref)

    @pl.when((step >= q_steps) & (step < q_steps + kv_steps))
    def _():
        rotated(project(wk_ref, bk_ref), k_ref)

    @pl.when(step >= q_steps + kv_steps)
    def _():
        v_ref[...] = project(wv_ref, bv_ref).astype(jnp.bfloat16)


def qkv_project(tokens, gain, bias, cos_tab, sin_tab, w_query, w_key, w_value, b_query, b_key, b_value, head_dim):
    rows, d_model = tokens.shape
    q_dim, kv_dim = w_query.shape[1], w_key.shape[1]
    block = 512
    q_steps, kv_steps = q_dim // block, kv_dim // block

    def q_idx(i):
        return (0, jnp.minimum(i, q_steps - 1))

    def k_idx(i):
        return (0, jnp.clip(i - q_steps, 0, kv_steps - 1))

    def v_idx(i):
        return (0, jnp.clip(i - q_steps - kv_steps, 0, kv_steps - 1))

    def whole(arr):
        return pl.BlockSpec(arr.shape, lambda i: (0,) * arr.ndim)

    gain, bias = gain[None, :], bias[None, :]
    return pl.pallas_call(
        functools.partial(qkv_kernel, head_dim, q_steps, kv_steps),
        grid=(q_steps + 2 * kv_steps,),
        in_specs=[
            whole(tokens), whole(gain), whole(bias), whole(cos_tab), whole(sin_tab),
            pl.BlockSpec((d_model, block), q_idx), pl.BlockSpec((d_model, block), k_idx), pl.BlockSpec((d_model, block), v_idx),
            pl.BlockSpec((1, block), q_idx), pl.BlockSpec((1, block), k_idx), pl.BlockSpec((1, block), v_idx),
        ],
        out_specs=[pl.BlockSpec((rows, block), q_idx), pl.BlockSpec((rows, block), k_idx), pl.BlockSpec((rows, block), v_idx)],
        out_shape=[jax.ShapeDtypeStruct((rows, q_dim), jnp.bfloat16), jax.ShapeDtypeStruct((rows, kv_dim), jnp.bfloat16), jax.ShapeDtypeStruct((rows, kv_dim), jnp.bfloat16)],
        scratch_shapes=[pltpu.VMEM((rows, d_model), jnp.bfloat16)],
        compiler_params=pltpu.CompilerParams(dimension_semantics=("arbitrary",), vmem_limit_bytes=40 * MIB),
        cost_estimate=pl.CostEstimate(flops=2 * rows * d_model * (q_dim + 2 * kv_dim), bytes_accessed=2 * d_model * (q_dim + 2 * kv_dim), transcendentals=0),
    )(tokens, gain, bias, cos_tab, sin_tab, w_query, w_key, w_value, b_query[None, :], b_key[None, :], b_value[None, :])


def attend_kernel(batch, ahead, kv_heads, group_size, pos_ref, q_ref, kn_ref, vn_ref, k_hbm, v_hbm, out_ref, k_buf, v_buf, where_ref, k_sem, v_sem):
    tok_count, seq_len = k_hbm.shape[0], k_hbm.shape[1]
    num_heads, head_dim = q_ref.shape[1], q_ref.shape[2]
    rounds = tok_count // batch
    slots = ahead + 1
    cols = seq_len * kv_heads
    v_buf[...] = jnp.zeros_like(v_buf)
    col_ids = lax.broadcasted_iota(jnp.int32, (num_heads, cols), 1)
    head_ids = lax.broadcasted_iota(jnp.int32, (num_heads, cols), 0)
    where_ref[...] = jnp.where(col_ids % kv_heads == head_ids // group_size, col_ids // kv_heads, seq_len)

    def copies(turn, lane):
        tok = turn * batch + lane
        slot = lax.rem(turn, slots)
        count = ((pos_ref[tok] + 7) // 8) * 8
        k_copy = pltpu.make_async_copy(k_hbm.at[tok, pl.ds(0, count)], k_buf.at[slot, lane, pl.ds(0, count)], k_sem.at[slot])
        v_copy = pltpu.make_async_copy(v_hbm.at[tok, pl.ds(0, count)], v_buf.at[slot, lane, pl.ds(0, count)], v_sem.at[slot])
        return k_copy, v_copy

    def fetch(turn):
        for lane in range(batch):
            for copy in copies(turn, lane):
                copy.start()

    for turn in range(ahead):
        fetch(turn)

    scale = head_dim ** -0.5

    def one_round(turn, carry):
        @pl.when(turn + ahead < rounds)
        def _():
            fetch(turn + ahead)

        slot = lax.rem(turn, slots)
        for lane in range(batch):
            for copy in copies(turn, lane):
                copy.wait()
        for lane in range(batch):
            tok = turn * batch + lane
            pos = pos_ref[tok]
            k_buf[slot, lane, pos] = kn_ref[tok]
            v_buf[slot, lane, pos] = vn_ref[tok]
        for lane in range(batch):
            tok = turn * batch + lane
            pos = pos_ref[tok]
            k_all = k_buf[slot, lane].reshape(cols, head_dim)
            v_all = v_buf[slot, lane].reshape(cols, head_dim)
            s_val = lax.dot_general(q_ref[tok], k_all, (((1,), (1,)), ((), ())), preferred_element_type=jnp.float32) * scale
            s_val = jnp.where(where_ref[...] <= pos, s_val, -jnp.inf)
            e_val = jnp.exp(s_val - jnp.max(s_val, axis=-1, keepdims=True))
            p_val = (e_val * (1.0 / jnp.sum(e_val, axis=-1, keepdims=True))).astype(jnp.bfloat16)
            out_ref[tok] = jnp.dot(p_val, v_all, preferred_element_type=jnp.float32).astype(jnp.bfloat16)
        return carry

    lax.fori_loop(0, rounds, one_round, 0)


def attend(positions, q_heads, key_new, value_new, k_cache, v_cache):
    tok_count, seq_len, kv_heads, head_dim = k_cache.shape
    num_heads = q_heads.shape[1]
    batch, ahead = 4, 3
    buf = pltpu.VMEM((ahead + 1, batch, seq_len, kv_heads, head_dim), jnp.bfloat16)
    vmem = pl.BlockSpec(memory_space=pltpu.VMEM)
    return pl.pallas_call(
        functools.partial(attend_kernel, batch, ahead, kv_heads, num_heads // kv_heads),
        in_specs=[pl.BlockSpec(memory_space=pltpu.SMEM), vmem, vmem, vmem, pl.BlockSpec(memory_space=pltpu.HBM), pl.BlockSpec(memory_space=pltpu.HBM)],
        out_specs=vmem,
        out_shape=jax.ShapeDtypeStruct(q_heads.shape, jnp.bfloat16),
        scratch_shapes=[buf, buf, pltpu.VMEM((num_heads, seq_len * kv_heads), jnp.int32), pltpu.SemaphoreType.DMA((ahead + 1,)), pltpu.SemaphoreType.DMA((ahead + 1,))],
        compiler_params=pltpu.CompilerParams(vmem_limit_bytes=32 * MIB),
        cost_estimate=pl.CostEstimate(flops=4 * tok_count * num_heads * seq_len * kv_heads * head_dim, bytes_accessed=4 * k_cache.size, transcendentals=0),
    )(positions, q_heads, key_new, value_new, k_cache, v_cache)


def post_kernel(num_experts, steps, attn_ref, wo_ref, bo_ref, tok_ref, gain_ref, bias_ref, wr_ref, one_ref, two_ref, elig_ref, x_ref, send_ref, acc_ref):
    step = pl.program_id(0)
    block = wo_ref.shape[1]
    cols = pl.ds(pl.multiple_of(step * block, block), block)
    mixed = jnp.dot(attn_ref[...], wo_ref[...], preferred_element_type=jnp.float32)
    x_mid = (tok_ref[...].astype(jnp.float32) + mixed + bo_ref[...].astype(jnp.float32)).astype(jnp.bfloat16)
    x_ref[...] = x_mid
    acc_ref[:, cols] = x_mid

    @pl.when(step == steps - 1)
    def _():
        h_two = layer_norm_rows(acc_ref[...].astype(jnp.float32), gain_ref[...].astype(jnp.float32), bias_ref[...].astype(jnp.float32)).astype(jnp.bfloat16)
        logits = jnp.dot(h_two, wr_ref[...], preferred_element_type=jnp.float32)
        rows, width = logits.shape
        lanes = lax.broadcasted_iota(jnp.int32, (rows, width), 1)
        hit_one = lanes == one_ref[...]
        hit_two = lanes == two_ref[...]
        keep_one = elig_ref[...] == 1
        keep_two = keep_one & jnp.logical_not(hit_one)

        def gate(keep, hit):
            masked = jnp.where(keep, logits, -jnp.inf)
            e_val = jnp.exp(masked - jnp.max(masked, axis=-1, keepdims=True))
            return jnp.sum(jnp.where(hit, e_val, 0.0), axis=-1, keepdims=True) / jnp.sum(e_val, axis=-1, keepdims=True)

        gates = jnp.where(hit_one, gate(keep_one, hit_one), 0.0) + jnp.where(hit_two, gate(keep_two, hit_two), 0.0)
        high = gates.astype(jnp.bfloat16).astype(jnp.float32)
        rest = gates - high
        mid = rest.astype(jnp.bfloat16).astype(jnp.float32)
        packed = high + pltpu.roll(mid, num_experts, 1) + pltpu.roll(rest - mid, 2 * num_experts, 1)
        d_model = h_two.shape[1]
        send_ref[:, :d_model] = h_two
        send_ref[:, d_model:] = packed.astype(jnp.bfloat16)


def post_attention(attn, w_out, b_out, tokens, gain, bias, w_router, expert_one, expert_two, eligible):
    rows, d_model = tokens.shape
    num_experts = w_router.shape[1]
    width = 128
    block = 512
    steps = d_model // block
    w_router = jnp.pad(w_router, ((0, 0), (0, width - num_experts)))
    eligible = jnp.pad(eligible, ((0, 0), (0, width - num_experts)))
    one, two = expert_one[:, None], expert_two[:, None]
    gain, bias = gain[None, :], bias[None, :]

    def whole(arr):
        return pl.BlockSpec(arr.shape, lambda i: (0,) * arr.ndim)

    def col(i):
        return (0, i)

    return pl.pallas_call(
        functools.partial(post_kernel, num_experts, steps),
        grid=(steps,),
        in_specs=[
            whole(attn), pl.BlockSpec((attn.shape[1], block), col), pl.BlockSpec((1, block), col), pl.BlockSpec((rows, block), col),
            whole(gain), whole(bias), whole(w_router), whole(one), whole(two), whole(eligible),
        ],
        out_specs=[pl.BlockSpec((rows, block), col), pl.BlockSpec((rows, d_model + width), lambda i: (0, 0))],
        out_shape=[jax.ShapeDtypeStruct((rows, d_model), jnp.bfloat16), jax.ShapeDtypeStruct((rows, d_model + width), jnp.bfloat16)],
        scratch_shapes=[pltpu.VMEM((rows, d_model), jnp.bfloat16)],
        compiler_params=pltpu.CompilerParams(dimension_semantics=("arbitrary",), vmem_limit_bytes=48 * MIB),
        cost_estimate=pl.CostEstimate(flops=2 * rows * d_model * d_model, bytes_accessed=2 * d_model * d_model, transcendentals=0),
    )(attn, w_out, b_out[None, :], tokens, gain, bias, w_router, one, two, eligible)


def expert_kernel(num_experts, x_ref, wg_ref, wu_ref, wd_ref, y_ref):
    d_model = y_ref.shape[1]
    me = lax.axis_index('ep')
    x_val = x_ref[:, :d_model]
    packed = x_ref[:, d_model:].astype(jnp.float32)
    lanes = lax.broadcasted_iota(jnp.int32, packed.shape, 1)
    gate = jnp.sum(jnp.where(lanes % num_experts == me, packed, 0.0), axis=-1, keepdims=True)
    u_val = jnp.dot(x_val, wg_ref[0], preferred_element_type=jnp.float32)
    v_val = jnp.dot(x_val, wu_ref[0], preferred_element_type=jnp.float32)
    z_val = (u_val * jax.nn.sigmoid(u_val) * v_val).astype(jnp.bfloat16)
    y_val = jnp.dot(z_val, wd_ref[0], preferred_element_type=jnp.float32).astype(jnp.bfloat16)
    y_ref[...] = gate * y_val.astype(jnp.float32)


def expert_mlp(rows_in, w_gate, w_up, w_down, num_experts):
    rows, width = rows_in.shape
    d_ff, d_model = w_down.shape[1:]
    tile = 256

    def fixed(arr):
        return pl.BlockSpec(arr.shape, lambda i: (0, 0, 0), pipeline_mode=pl.Buffered(1))

    return pl.pallas_call(
        functools.partial(expert_kernel, num_experts),
        grid=(rows // tile,),
        in_specs=[pl.BlockSpec((tile, width), lambda i: (i, 0)), fixed(w_gate), fixed(w_up), fixed(w_down)],
        out_specs=pl.BlockSpec((tile, d_model), lambda i: (i, 0)),
        out_shape=jax.ShapeDtypeStruct((rows, d_model), jnp.float32),
        compiler_params=pltpu.CompilerParams(dimension_semantics=("arbitrary",), vmem_limit_bytes=52 * MIB),
        cost_estimate=pl.CostEstimate(flops=6 * rows * d_model * d_ff, bytes_accessed=6 * d_model * d_ff, transcendentals=0),
    )(rows_in, w_gate, w_up, w_down)


def solution(mesh):
    def local_step(tokens, k_cache, v_cache, positions, expert_one, expert_two, eligible, ln1_gain, ln1_bias, w_query, b_query, w_key, b_key, w_value, b_value, w_out, b_out, ln2_gain, ln2_bias, w_router, w_gate, w_up, w_down):
        rows, d_model = tokens.shape
        _, seq_len, kv_heads, head_dim = k_cache.shape
        num_heads = w_query.shape[1] // head_dim
        num_experts = w_router.shape[1]
        cos_tab, sin_tab = rope_tables(positions, head_dim)
        q_flat, k_flat, v_flat = qkv_project(tokens, ln1_gain, ln1_bias, cos_tab, sin_tab, w_query, w_key, w_value, b_query, b_key, b_value, head_dim)
        key_new = k_flat.reshape(rows, kv_heads, head_dim)
        value_new = v_flat.reshape(rows, kv_heads, head_dim)
        attn = attend(positions, q_flat.reshape(rows, num_heads, head_dim), key_new, value_new, k_cache, v_cache)
        x_mid, send = post_attention(attn.reshape(rows, num_heads * head_dim), w_out, b_out, tokens, ln2_gain, ln2_bias, w_router, expert_one, expert_two, eligible)
        chunk = rows // CHUNKS
        arrived = [lax.all_gather(send[c * chunk:(c + 1) * chunk], 'ep', axis=0, tiled=True) for c in range(CHUNKS)]
        outs = []
        for c in range(CHUNKS):
            partial = expert_mlp(arrived[c], w_gate, w_up, w_down, num_experts)
            y_sum = lax.psum_scatter(partial, 'ep', scatter_dimension=0, tiled=True)
            outs.append((x_mid[c * chunk:(c + 1) * chunk].astype(jnp.float32) + y_sum).astype(jnp.bfloat16))
        tokens_out = jnp.concatenate(outs, axis=0)
        return tokens_out, key_new, value_new

    row_spec = P('ep', None)
    cache_spec = P('ep', None, None, None)
    vec_spec = P('ep')
    rep_one = P(None)
    rep_two = P(None, None)
    expert_spec = P('ep', None, None)
    in_specs = (row_spec, cache_spec, cache_spec, vec_spec, vec_spec, vec_spec, row_spec, rep_one, rep_one, rep_two, rep_one, rep_two, rep_one, rep_two, rep_one, rep_two, rep_one, rep_one, rep_one, rep_two, expert_spec, expert_spec, expert_spec)
    out_specs = (row_spec, expert_spec, expert_spec)
    return jax.shard_map(local_step, mesh=mesh, in_specs=in_specs, out_specs=out_specs, check_vma=False)
```

time: 644 us -> 589 us (0.915); the launches traced: 635 us -> 588 us
  blocking collectives: 192 us -> 0 us
  Pallas kernels: 0 us -> 172 us
  waiting for transfers between devices: 205 us -> 363 us
  matrix products: 153 us -> 0 us
  other arithmetic: 28.9 us -> 3.86 us
  local copies, waits for them, and re-layouts: 51.6 us -> 34.8 us
  between operations: 1.53 us -> 14.1 us
    reduce_scatter x0 -> x2, waiting for transfers between devices: none -> 320 us  [local_step(): y_sum = lax.psum_scatter(partial, 'ep', scatter_dimension=0, tiled=True)]
    all_to_all x1 -> x0, waiting for transfers between devices: 205 us -> none  [local_step(): lax.all_to_all(expert_out.reshape(local_experts, groups, tok_count, d_mod...]
    all_to_all x1 -> x0, blocking collectives: 192 us -> none  [local_step(): recv_rows = lax.all_to_all(send_rows, 'ep', 1, 1, tiled=True)]
    pallas_call x0 -> x5, Pallas kernels: none -> 172 us  [the longest x2 74.9 us: expert_mlp(): pl.pallas_call(functools.partial(expert_kernel, num_experts), grid=(rows...]
    dot_general x11 -> x0, matrix products: 153 us -> none  [the longest x1 23.9 us: expert_mlp(): jnp.einsum('emf,efd->emd', z_val, w_down, preferred_element_type=jnp.floa...]
    all_gather x0 -> x2, waiting for transfers between devices: none -> 42 us  [local_step(): lax.all_gather(send[c * chunk:(c + 1) * chunk], 'ep', axis=0, tiled=True)]
    gather x3 -> x0, local copies, waits for them, and re-layouts: 35.7 us -> none  [the longest x1 14.3 us: local_step(): jnp.take(h_two, src_token, axis=0)]
    unnamed x50 -> x34, local copies, waits for them, and re-layouts: 4.97 us -> 29.7 us
  transfers between devices with their start and end apart: 1 -> 4, of which waited for: 1 -> 4; matrix products, arithmetic and copies ran while one was open for 0% -> 4% of each run, Pallas kernels for 0% -> 13%
where the time goes in v1:
time: 589 us; the launch traced here: 588 us
  waiting for transfers between devices  363 us (62%)
  Pallas kernels  172 us (29%)
  local copies, waits for them, and re-layouts  34.8 us (6%)
  between operations  14.1 us (2%)
    reduce_scatter x2, waiting for transfers between devices, local_step(): y_sum = lax.psum_scatter(partial, 'ep', scatter_dimension=0, tiled=True)  320 us
    pallas_call x2, Pallas kernels, expert_mlp(): pl.pallas_call(functools.partial(expert_kernel, num_experts), grid=(rows...  74.9 us
    pallas_call x1, Pallas kernels, attend(): pl.pallas_call(functools.partial(attend_kernel, batch, ahead, kv_heads, n...  60.3 us
    all_gather x2, waiting for transfers between devices, local_step(): lax.all_gather(send[c * chunk:(c + 1) * chunk], 'ep', axis=0, tiled=True)  42 us
    unnamed x34, local copies, waits for them, and re-layouts  29.7 us
    pallas_call x1, Pallas kernels, qkv_project(): pl.pallas_call(functools.partial(qkv_kernel, head_dim, q_steps, kv_steps)...  22 us
    pallas_call x1, Pallas kernels, post_attention(): pl.pallas_call(functools.partial(post_kernel, num_experts, steps), grid=(...  15 us
  transfers between devices with their start and end apart: 4, of which 4 were waited for; matrix products, arithmetic and copies ran while one was open for 4% of the time, Pallas kernels for 13%

profile of v1, /device:TPU:0, one launch (start us, length us, event | category | flops | bytes accessed | tf_op | source)
XLA Modules:
  0.0 587.7 jit_solution(14058705880802516367)
XLA Ops:
  7.2 0.0 all-gather.3.cloned.1.call-start
  7.2 0.7 broadcast_in_dim.32.gain_ref
  7.9 0.7 broadcast_in_dim.33.bias_ref
  8.7 0.7 convert_element_type.17
  9.3 0.7 broadcast_in_dim.34.bq_ref
  10.0 0.7 broadcast_in_dim.35.bk_ref
  10.7 0.7 broadcast_in_dim.36.bv_ref
  11.4 0.3 fusion
  11.7 0.1 pad_maximum_fusion.1
  11.8 0.0 copy-start
  11.8 3.4 copy-done
  15.2 1.2 copy-done.1
  16.4 22.0 %shard_map.238 = (bf16[128,4096]{1,0:T(8,128)(2,1)S(1)}, bf16[128,1024]{1,0:T(8,128)(2,1)S(1)}, bf16[128,1024]{1,0:T(8,128)(2,1)S(1)}) custom-call(bf16[128,4096]{1,0:T(8,128)(2,1)S(1)} %copy-done.1, bf16[1,4096]{1,0:T(2,128)(2,1)S(1)} %broadcast_in_dim.32.gain_ref, bf16[1,4096]{1,0:T(2,128)(2,1)S(1)} %broadcast_in_dim.33.bias_ref, ...), custom_call_target="tpu_custom_call" | custom-call | flops 6442450944 | bytes 50331648 | tf_op jit(solution)/shard_map/pallas_call | solution.py:81
  38.4 0.2 copy.34
  38.7 0.0 copy-start.3
  38.8 0.0 copy-start.4
  38.8 0.0 copy-start.7
  38.8 0.0 copy-start.8
  38.9 0.0 copy-start.9
  38.9 0.0 copy-start.6
  38.9 0.0 copy-start.11
  38.9 0.0 copy-start.12
  38.9 60.3 %shard_map.239 = bf16[128,32,128]{2,1,0:T(8,128)(2,1)S(1)} custom-call(s32[128]{0:T(128)S(1)} %copy-done.5, bf16[128,32,128]{2,1,0:T(8,128)(2,1)S(1)} %bitcast.13, bf16[128,8,128]{2,1,0:T(8,128)(2,1)S(1)} %bitcast.15, bf16[128,8,128]{2,1,0:T(8,128)(2,1)S(1)} %bitcast.17, bf16[128,128,8,128]{3,2,1,0:T(8,128)(2,1)} %k_hbm.1, bf16[128,128,8,128]{3,2,1,0:T(8,128)(2,1)} %v_hbm.1), custom_call_target="tpu_custom_call" | custom-call | flops 2147483648 | bytes 67108864 | tf_op jit(solution)/shard_map/pallas_call | solution.py:161
  99.3 0.5 copy.39
  99.8 0.5 copy.26
  100.3 0.1 copy.28.one_ref
  100.4 0.1 copy.29.two_ref
  100.5 0.1 copy.27
  100.6 0.2 pad.8.wr_ref
  100.9 15.0 %shard_map.240 = (bf16[128,4096]{1,0:T(8,128)(2,1)S(1)}, bf16[128,4224]{1,0:T(8,128)(2,1)S(1)}) custom-call(bf16[128,4096]{1,0:T(8,128)(2,1)S(1)} %bitcast.12, bf16[4096,4096]{1,0:T(8,128)(2,1)} %wo_ref.1, bf16[1,4096]{1,0:T(2,128)(2,1)S(1)} %broadcast_in_dim.37.bo_ref, bf16[128,4096]{1,0:T(8,128)(2,1)S(1)} %copy-done.2, ...), custom_call_target="tpu_custom_call" | custom-call | flops 4294967296 | bytes 33554432 | tf_op jit(solution)/shard_map/pallas_call | solution.py:224
  115.9 1.1 fusion.1
  117.0 0.0 all-gather.3.cloned.1.call-update
  117.0 0.0 all-gather.5.cloned.1.call-start
  117.0 0.7 all-gather.5.cloned.1.call-update
  117.7 0.2 reduce-scatter.3.cloned.1.call-start
  118.0 11.8 %copy.30.wg_ref = bf16[1,4096,960]{2,1,0:T(8,128)(2,1)} copy(bf16[1,4096,960]{1,2,0:T(8,128)(2,1)} %param.43) | data formatting | bytes 15728640 | tf_op args[20]
  129.8 11.8 %copy.31.wu_ref = bf16[1,4096,960]{2,1,0:T(8,128)(2,1)} copy(bf16[1,4096,960]{1,2,0:T(8,128)(2,1)} %param.44) | data formatting | bytes 15728640 | tf_op args[21]
  141.6 27.8 %all-gather.3.cloned.1.call-done.x_ref = bf16[1024,4224]{1,0:T(8,128)(2,1)} async-done(((bf16[64,4224]{1,0:T(8,128)(2,1)}), bf16[1024,4224]{1,0:T(8,128)(2,1)}) %all-gather.3.cloned.1.call-update) | async-done | bytes 8650768 | tf_op jit(solution)/shard_map/all_gather | solution.py:285
  169.4 37.4 %shard_map.241 = f32[1024,4096]{1,0:T(8,128)} custom-call(bf16[1024,4224]{1,0:T(8,128)(2,1)} %all-gather.3.cloned.1.call-done.x_ref, bf16[1,4096,960]{2,1,0:T(8,128)(2,1)} %copy.30.wg_ref, bf16[1,4096,960]{2,1,0:T(8,128)(2,1)} %copy.31.wu_ref, bf16[1,960,4096]{2,1,0:T(8,128)(2,1)} %wd_ref.3), custom_call_target="tpu_custom_call" | custom-call | flops 24159191040 | bytes 23592960 | tf_op jit(solution)/shard_map/pallas_call | solution.py:261
  206.8 0.0 reduce-scatter.3.cloned.1.call-update
  206.9 0.0 reduce-scatter.5.cloned.1.call-start
  206.9 14.2 %all-gather.5.cloned.1.call-done.x_ref = bf16[1024,4224]{1,0:T(8,128)(2,1)} async-done(((bf16[64,4224]{1,0:T(8,128)(2,1)}), bf16[1024,4224]{1,0:T(8,128)(2,1)}) %all-gather.5.cloned.1.call-update) | async-done | bytes 8650768 | tf_op jit(solution)/shard_map/all_gather | solution.py:285
  221.1 37.4 %shard_map.242 = f32[1024,4096]{1,0:T(8,128)} custom-call(bf16[1024,4224]{1,0:T(8,128)(2,1)} %all-gather.5.cloned.1.call-done.x_ref, bf16[1,4096,960]{2,1,0:T(8,128)(2,1)} %copy.30.wg_ref, bf16[1,4096,960]{2,1,0:T(8,128)(2,1)} %copy.31.wu_ref, bf16[1,960,4096]{2,1,0:T(8,128)(2,1)} %wd_ref.3), custom_call_target="tpu_custom_call" | custom-call | flops 24159191040 | bytes 23592960 | tf_op jit(solution)/shard_map/pallas_call | solution.py:261
  258.6 0.0 reduce-scatter.5.cloned.1.call-update
  258.6 142.1 %reduce-scatter.3.cloned.1.call-done = f32[64,4096]{1,0:T(8,128)} async-done(((f32[1024,4096]{1,0:T(8,128)}), f32[64,4096]{1,0:T(8,128)}) %reduce-scatter.3.cloned.1.call-update) | async-done | bytes 1048592 | tf_op jit(solution)/shard_map/reduce_scatter | solution.py:289
  400.8 177.6 %reduce-scatter.5.cloned.1.call-done = f32[64,4096]{1,0:T(8,128)} async-done(((f32[1024,4096]{1,0:T(8,128)}), f32[64,4096]{1,0:T(8,128)}) %reduce-scatter.5.cloned.1.call-update) | async-done | bytes 1048592 | tf_op jit(solution)/shard_map/reduce_scatter | solution.py:289
  578.4 1.7 add_convert_fusion.1
  580.1 1.0 pad_maximum_fusion
  (22 shorter events, 0.2 us)
Async XLA Ops:
  7.2 162.2 %all-gather.3.cloned.1.call-start = ((), (), s32[]{:S(2)}) async-start(), calls=%async_computation.2 | async-start | bytes 9191424 | tf_op jit(solution)/shard_map/all_gather | solution.py:285
  11.8 3.4 copy-start
  15.2 1.2 copy-start.1
  16.4 22.4 %copy-start.5 = (s32[128]{0:T(128)S(1)}, s32[128]{0:T(128)}, u32[]{:S(2)}) copy-start(s32[128]{0:T(128)} %pos_ref.1) | copy-start | bytes 1540
  38.7 60.5 %copy-start.3 = (bf16[16,8,8,128]{3,2,1,0:T(8,128)(2,1)}, bf16[16,8,8,128]{3,2,1,0:T(8,128)(2,1)S(1)}, u32[]{:S(2)}) copy-start(bf16[16,8,8,128]{3,2,1,0:T(8,128)(2,1)S(1)} %copy.35) | copy-start | bytes 786436
  38.8 60.4 %copy-start.4 = (bf16[16,8,8,128]{3,2,1,0:T(8,128)(2,1)}, bf16[16,8,8,128]{3,2,1,0:T(8,128)(2,1)S(1)}, u32[]{:S(2)}) copy-start(bf16[16,8,8,128]{3,2,1,0:T(8,128)(2,1)S(1)} %copy.36) | copy-start | bytes 786436
  38.8 60.9 %copy-start.7 = (bf16[4096]{0:T(1024)(128)(2,1)S(1)}, bf16[4096]{0:T(1024)(128)(2,1)}, u32[]{:S(2)}) copy-start(bf16[4096]{0:T(1024)(128)(2,1)} %param.39) | copy-start | bytes 24580
  38.8 60.9 %copy-start.8 = (bf16[4096]{0:T(1024)(128)(2,1)S(1)}, bf16[4096]{0:T(1024)(128)(2,1)}, u32[]{:S(2)}) copy-start(bf16[4096]{0:T(1024)(128)(2,1)} %param.40) | copy-start | bytes 24580
  38.9 60.9 %copy-start.9 = (bf16[4096]{0:T(1024)(128)(2,1)S(1)}, bf16[4096]{0:T(1024)(128)(2,1)}, u32[]{:S(2)}) copy-start(bf16[4096]{0:T(1024)(128)(2,1)} %param.41) | copy-start | bytes 24580
  38.9 60.9 %copy-start.6 = (bf16[4096,16]{0,1:T(8,128)(2,1)S(1)}, bf16[4096,16]{0,1:T(8,128)(2,1)}, u32[]{:S(2)}) copy-start(bf16[4096,16]{0,1:T(8,128)(2,1)} %param.42) | copy-start | bytes 393220
  38.9 61.4 %copy-start.11 = (s32[128]{0:T(128)S(1)}, s32[128]{0:T(128)}, u32[]{:S(2)}) copy-start(s32[128]{0:T(128)} %param.27) | copy-start | bytes 1540
  38.9 61.5 %copy-start.12 = (s32[128]{0:T(128)S(1)}, s32[128]{0:T(128)}, u32[]{:S(2)}) copy-start(s32[128]{0:T(128)} %param.28) | copy-start | bytes 1540
  38.9 61.6 %copy-start.10 = (s32[128,16]{0,1:T(8,128)S(1)}, s32[128,16]{0,1:T(8,128)}, u32[]{:S(2)}) copy-start(s32[128,16]{0,1:T(8,128)} %param.29) | copy-start | bytes 24580
  38.9 62.0 %copy-start.2 = (bf16[128,4096]{1,0:T(8,128)(2,1)S(1)}, bf16[128,4096]{1,0:T(8,128)(2,1)}, u32[]{:S(2)}) copy-start(bf16[128,4096]{1,0:T(8,128)(2,1)} %tok_ref.3) | copy-start | bytes 3145732
  117.0 104.2 %all-gather.5.cloned.1.call-start = ((), (), s32[]{:S(2)}) async-start(), calls=%async_computation.4 | async-start | bytes 9191424 | tf_op jit(solution)/shard_map/all_gather | solution.py:285
  117.7 283.0 %reduce-scatter.3.cloned.1.call-start = ((), (), s32[]{:S(2)}) async-start(), calls=%async_computation.3 | async-start | bytes 17825792 | tf_op jit(solution)/shard_map/reduce_scatter | solution.py:289
  206.9 371.5 %reduce-scatter.5.cloned.1.call-start = ((), (), s32[]{:S(2)}) async-start(), calls=%async_computation.5 | async-start | bytes 17825792 | tf_op jit(solution)/shard_map/reduce_scatter | solution.py:289
Sparse Core Ops, SparseCore 0:
  117.1 52.2 all-gather.2
  171.6 49.4 all-gather.4
  223.4 177.2 reduce-scatter.2
  402.9 175.4 reduce-scatter.4

commit v2 on v1

--- a/solution.py
+++ b/solution.py
@@ -9,7 +9,6 @@
 
 ROPE_BASE = 10000.0
 LN_EPS = 1e-5
-CHUNKS = 2
 MIB = 1024 * 1024
 
 
@@ -236,37 +235,275 @@
     )(attn, w_out, b_out[None, :], tokens, gain, bias, w_router, one, two, eligible)
 
 
-def expert_kernel(num_experts, x_ref, wg_ref, wu_ref, wd_ref, y_ref):
-    d_model = y_ref.shape[1]
+STEP_ROWS = 16
+DIMS = 3
+
+
+def moe_kernel(num_experts, h_ref, xm_ref, wg_hbm, wu_hbm, wd_hbm, out_ref, all_ref, wg_ref, wu_ref, wd_ref, x_buf, y_buf, mate_buf, keep_refs, send_refs, recv_refs, w_sem, x_sem, own_sem, gs_sem, gr_sem, ms_sem, mr_sem, mate_s, mate_r, mate_free, red_s, red_r, red_free):
     me = lax.axis_index('ep')
-    x_val = x_ref[:, :d_model]
-    packed = x_ref[:, d_model:].astype(jnp.float32)
-    lanes = lax.broadcasted_iota(jnp.int32, packed.shape, 1)
-    gate = jnp.sum(jnp.where(lanes % num_experts == me, packed, 0.0), axis=-1, keepdims=True)
-    u_val = jnp.dot(x_val, wg_ref[0], preferred_element_type=jnp.float32)
-    v_val = jnp.dot(x_val, wu_ref[0], preferred_element_type=jnp.float32)
-    z_val = (u_val * jax.nn.sigmoid(u_val) * v_val).astype(jnp.bfloat16)
-    y_val = jnp.dot(z_val, wd_ref[0], preferred_element_type=jnp.float32).astype(jnp.bfloat16)
-    y_ref[...] = gate * y_val.astype(jnp.float32)
-
-
-def expert_mlp(rows_in, w_gate, w_up, w_down, num_experts):
-    rows, width = rows_in.shape
+    core = lax.rem(me, 2)
+    chip = me // 2
+    mate = chip * 2 + 1 - core
+    rows, d_model = xm_ref.shape
+    width = h_ref.shape[1]
+    third = width // 3
+    chunks = rows // STEP_ROWS
+    logical = pl.DeviceIdType.MESH
+
+    def bit(dim):
+        return (chip // (1 << dim)) % 2
+
+    def across(who, dim):
+        return who + (1 - 2 * ((who // (1 << dim)) % 2)) * (1 << dim)
+
+    def device_of(who):
+        return who * 2 + core
+
+    peers = [device_of(across(chip, dim)) for dim in range(DIMS)]
+
+    weights = [pltpu.make_async_copy(src.at[0], dst, w_sem.at[n]) for n, (src, dst) in enumerate(((wg_hbm, wg_ref), (wu_hbm, wu_ref), (wd_hbm, wd_ref)))]
+    for copy in weights:
+        copy.start()
+    own = pltpu.make_async_copy(h_ref, all_ref.at[me], own_sem)
+    own.start()
+
+    barrier = pltpu.get_barrier_semaphore()
+    for peer in peers + [mate]:
+        pl.semaphore_signal(barrier, inc=1, device_id=(peer,), device_id_type=logical)
+    pl.semaphore_wait(barrier, DIMS + 1)
+
+    def piece(owner, part, mine):
+        cols = pl.ds(part * third, third)
+        src = h_ref.at[:, cols] if mine else all_ref.at[owner, :, cols]
+        return src, all_ref.at[owner, :, cols]
+
+    def spread(owner, part, slot, peer, mine):
+        src, dst = piece(owner, part, mine)
+        return pltpu.make_async_remote_copy(src, dst, gs_sem.at[part, slot], gr_sem.at[part, slot], device_id=(peer,), device_id_type=logical)
+
+    def share(owner, part, slot, mine):
+        src, dst = piece(owner, part, mine)
+        return pltpu.make_async_remote_copy(src, dst, ms_sem.at[part, slot], mr_sem.at[part, slot], device_id=(mate,), device_id_type=logical)
+
+    started = []
+    for part in range(3):
+        copy = share(me, part, 0, True)
+        copy.start()
+        started.append(copy)
+    held = [[chip] for _ in range(3)]
+    base = 0
+    for step in range(DIMS):
+        wave = []
+        for part in range(3):
+            dim = (part + step) % 3
+            for n, who in enumerate(held[part]):
+                copy = spread(device_of(who), part, base + n, peers[dim], n == 0)
+                copy.start()
+                wave.append(copy)
+                started.append(copy)
+        for part in range(3):
+            dim = (part + step) % 3
+            count = len(held[part])
+            fresh = [across(who, dim) for who in held[part]]
+            for n, who in enumerate(fresh):
+                wave[part * count + n].wait_recv()
+                copy = share(device_of(who), part, 1 + base + n, False)
+                copy.start()
+                started.append(copy)
+            held[part] = held[part] + fresh
+        base += 1 << step
+    for copy in weights:
+        copy.wait()
+    own.wait()
+    for part in range(3):
+        for slot in range(8):
+            share(me, part, slot, True).wait_recv()
+    for copy in started:
+        copy.wait_send()
+
+    spans = []
+    at = 0
+    for ref in keep_refs[:3]:
+        spans.append((at, ref.shape[-1]))
+        at += ref.shape[-1]
+
+    def x_copy(c):
+        return pltpu.make_async_copy(all_ref.at[:, pl.ds(pl.multiple_of(c * STEP_ROWS, STEP_ROWS), STEP_ROWS)], x_buf, x_sem)
+
+    def mate_copy(c):
+        slot = lax.rem(c, 2)
+        return pltpu.make_async_remote_copy(y_buf.at[slot, :, 1 - core], mate_buf.at[slot], mate_s.at[slot], mate_r.at[slot], device_id=(mate,), device_id_type=logical)
+
+    def red_copy(c, level, part):
+        slot = lax.rem(c, 2)
+        n = level * 3 + part
+        return pltpu.make_async_remote_copy(send_refs[n].at[slot], recv_refs[n].at[slot], red_s.at[n, slot], red_r.at[n, slot], device_id=(peers[(part + level) % 3],), device_id_type=logical)
+
+    def experts(c):
+        slot = lax.rem(c, 2)
+        x_copy(c).wait()
+
+        @pl.when(c >= 2)
+        def _():
+            mate_copy(c - 2).wait_send()
+
+        x_all = x_buf[...].reshape(num_experts * STEP_ROWS, width)
+        packed = x_all[:, d_model:].astype(jnp.float32)
+        lanes = lax.broadcasted_iota(jnp.int32, packed.shape, 1)
+        gate = jnp.sum(jnp.where(lanes % num_experts == me, packed, 0.0), axis=-1, keepdims=True)
+        x_val = x_all[:, :d_model]
+        flat = (((1,), (1,)), ((), ()))
+        u_val = lax.dot_general(x_val, wg_ref[...], flat, preferred_element_type=jnp.float32)
+        v_val = lax.dot_general(x_val, wu_ref[...], flat, preferred_element_type=jnp.float32)
+        z_val = (u_val * jax.nn.sigmoid(u_val) * v_val).astype(jnp.bfloat16)
+        block = 1024
+        for n in range(d_model // block):
+            cols = slice(n * block, (n + 1) * block)
+            y_val = jnp.dot(z_val, wd_ref[:, cols], preferred_element_type=jnp.float32).astype(jnp.bfloat16)
+            y_buf[slot, :, :, :, cols] = (gate * y_val.astype(jnp.float32)).reshape(num_experts // 2, 2, STEP_ROWS, block)
+
+        @pl.when(c >= 2)
+        def _():
+            pl.semaphore_wait(mate_free, 1)
+
+        mate_copy(c).start()
+
+        @pl.when(c + 1 < chunks)
+        def _():
+            x_copy(c + 1).start()
+
+    def give(c, level):
+        for part in range(3):
+            @pl.when(c >= 2)
+            def _():
+                pl.semaphore_wait(red_free.at[level * 3 + part], 1)
+
+            red_copy(c, level, part).start()
+
+    def drained(c, level):
+        @pl.when(c >= 2)
+        def _():
+            for part in range(3):
+                red_copy(c - 2, level, part).wait_send()
+
+    def first(c):
+        slot = lax.rem(c, 2)
+        mate_copy(c).wait_recv()
+        drained(c, 0)
+        for part in range(3):
+            lo, size = spans[part]
+            cols = slice(lo, lo + size)
+            dims = [(part + k) % 3 for k in range(3)]
+            for n in range(4):
+                rest = (n % 2) * (1 << dims[1]) + (n // 2) * (1 << dims[2])
+                for side, refs in ((bit(dims[0]), keep_refs), (1 - bit(dims[0]), send_refs)):
+                    who = rest + side * (1 << dims[0])
+                    refs[part][slot, n] = y_buf[slot, who, core, :, cols] + mate_buf[slot, who, :, cols]
+
+        @pl.when(c + 2 < chunks)
+        def _():
+            pl.semaphore_signal(mate_free, inc=1, device_id=(mate,), device_id_type=logical)
+
+        give(c, 0)
+
+    def later(c, level):
+        slot = lax.rem(c, 2)
+        old, new = (level - 1) * 3, level * 3
+        drained(c, level)
+        for part in range(3):
+            red_copy(c, level - 1, part).wait_recv()
+            dim = (part + level) % 3
+            for n in range(1 << (2 - level)):
+                for side, refs in ((bit(dim), keep_refs), (1 - bit(dim), send_refs)):
+                    at = n * 2 + side
+                    refs[new + part][slot, n] = keep_refs[old + part][slot, at] + recv_refs[old + part][slot, at]
+
+            @pl.when(c + 2 < chunks)
+            def _():
+                pl.semaphore_signal(red_free.at[old + part], inc=1, device_id=(peers[(part + level - 1) % 3],), device_id_type=logical)
+
+        give(c, level)
+
+    def last(c):
+        slot = lax.rem(c, 2)
+        here = pl.ds(pl.multiple_of(c * STEP_ROWS, STEP_ROWS), STEP_ROWS)
+        for part in range(3):
+            red_copy(c, 2, part).wait_recv()
+            lo, size = spans[part]
+            cols = slice(lo, lo + size)
+            y_sum = keep_refs[6 + part][slot, 0] + recv_refs[6 + part][slot, 0]
+            out_ref[here, cols] = (xm_ref[here, cols].astype(jnp.float32) + y_sum).astype(jnp.bfloat16)
+
+            @pl.when(c + 2 < chunks)
+            def _():
+                pl.semaphore_signal(red_free.at[6 + part], inc=1, device_id=(peers[(part + 2) % 3],), device_id_type=logical)
+
+    x_copy(0).start()
+
+    def turn(i, carry):
+        @pl.when(i < chunks)
+        def _():
+            experts(i)
+
+        @pl.when((i >= 1) & (i - 1 < chunks))
+        def _():
+            first(i - 1)
+
+        @pl.when(i >= 4)
+        def _():
+            last(i - 4)
+
+        @pl.when((i >= 3) & (i - 3 < chunks))
+        def _():
+            later(i - 3, 2)
+
+        @pl.when((i >= 2) & (i - 2 < chunks))
+        def _():
+            later(i - 2, 1)
+
+        return carry
+
+    lax.fori_loop(0, chunks + 4, turn, 0)
+    for c in (chunks - 2, chunks - 1):
+        mate_copy(c).wait_send()
+        for level in range(3):
+            for part in range(3):
+                red_copy(c, level, part).wait_send()
+
+
+def moe_layer(h_rows, x_mid, w_gate, w_up, w_down, num_experts):
+    rows, width = h_rows.shape
     d_ff, d_model = w_down.shape[1:]
-    tile = 256
-
-    def fixed(arr):
-        return pl.BlockSpec(arr.shape, lambda i: (0, 0, 0), pipeline_mode=pl.Buffered(1))
-
-    return pl.pallas_call(
-        functools.partial(expert_kernel, num_experts),
-        grid=(rows // tile,),
-        in_specs=[pl.BlockSpec((tile, width), lambda i: (i, 0)), fixed(w_gate), fixed(w_up), fixed(w_down)],
-        out_specs=pl.BlockSpec((tile, d_model), lambda i: (i, 0)),
-        out_shape=jax.ShapeDtypeStruct((rows, d_model), jnp.float32),
-        compiler_params=pltpu.CompilerParams(dimension_semantics=("arbitrary",), vmem_limit_bytes=52 * MIB),
-        cost_estimate=pl.CostEstimate(flops=6 * rows * d_model * d_ff, bytes_accessed=6 * d_model * d_ff, transcendentals=0),
-    )(rows_in, w_gate, w_up, w_down)
+    unit = d_model // 128
+    sizes = [128 * (unit // 3 + (1 if part < unit % 3 else 0)) for part in range(3)]
+    chips = num_experts // 2
+    f32 = jnp.float32
+
+    def level_bufs():
+        return [pltpu.VMEM((2, chips >> (level + 1), STEP_ROWS, sizes[part]), f32) for level in range(3) for part in range(3)]
+
+    vmem = pl.BlockSpec(memory_space=pltpu.VMEM)
+    hbm = pl.BlockSpec(memory_space=pltpu.HBM)
+    dma = pltpu.SemaphoreType.DMA
+    regular = pltpu.SemaphoreType.REGULAR
+    out, _ = pl.pallas_call(
+        functools.partial(moe_kernel, num_experts),
+        in_specs=[vmem, vmem, hbm, hbm, hbm],
+        out_specs=[vmem, hbm],
+        out_shape=[jax.ShapeDtypeStruct((rows, d_model), jnp.bfloat16), jax.ShapeDtypeStruct((num_experts, rows, width), jnp.bfloat16)],
+        scratch_shapes=[
+            pltpu.VMEM((d_ff, d_model), jnp.bfloat16), pltpu.VMEM((d_ff, d_model), jnp.bfloat16), pltpu.VMEM((d_ff, d_model), jnp.bfloat16),
+            pltpu.VMEM((num_experts, STEP_ROWS, width), jnp.bfloat16),
+            pltpu.VMEM((2, chips, 2, STEP_ROWS, d_model), f32),
+            pltpu.VMEM((2, chips, STEP_ROWS, d_model), f32),
+            level_bufs(), level_bufs(), level_bufs(),
+            dma((3,)), dma, dma, dma((3, 7)), dma((3, 7)), dma((3, 8)), dma((3, 8)),
+            dma((2,)), dma((2,)), regular, dma((9, 2)), dma((9, 2)), regular((9,)),
+        ],
+        compiler_params=pltpu.CompilerParams(collective_id=0, has_side_effects=True, vmem_limit_bytes=67043328),
+        cost_estimate=pl.CostEstimate(flops=6 * rows * num_experts * d_model * d_ff, bytes_accessed=6 * d_model * d_ff, transcendentals=0),
+    )(h_rows, x_mid, jnp.swapaxes(w_gate, 1, 2), jnp.swapaxes(w_up, 1, 2), w_down)
+    return out
 
 
 def solution(mesh):
@@ -281,14 +518,7 @@
         value_new = v_flat.reshape(rows, kv_heads, head_dim)
         attn = attend(positions, q_flat.reshape(rows, num_heads, head_dim), key_new, value_new, k_cache, v_cache)
         x_mid, send = post_attention(attn.reshape(rows, num_heads * head_dim), w_out, b_out, tokens, ln2_gain, ln2_bias, w_router, expert_one, expert_two, eligible)
-        chunk = rows // CHUNKS
-        arrived = [lax.all_gather(send[c * chunk:(c + 1) * chunk], 'ep', axis=0, tiled=True) for c in range(CHUNKS)]
-        outs = []
-        for c in range(CHUNKS):
-            partial = expert_mlp(arrived[c], w_gate, w_up, w_down, num_experts)
-            y_sum = lax.psum_scatter(partial, 'ep', scatter_dimension=0, tiled=True)
-            outs.append((x_mid[c * chunk:(c + 1) * chunk].astype(jnp.float32) + y_sum).astype(jnp.bfloat16))
-        tokens_out = jnp.concatenate(outs, axis=0)
+        tokens_out = moe_layer(send, x_mid, w_gate, w_up, w_down, num_experts)
         return tokens_out, key_new, value_new
 
     row_spec = P('ep', None)

time: 589 us -> 320 us (0.54)
  waiting for transfers between devices: 363 us -> 0 us
  Pallas kernels: 172 us -> 298 us
  local copies, waits for them, and re-layouts: 34.8 us -> 19.2 us
  between operations: 14.1 us -> 0.82 us
    reduce_scatter x2 -> x0, waiting for transfers between devices: 320 us -> none  [local_step(): y_sum = lax.psum_scatter(partial, 'ep', scatter_dimension=0, tiled=True)]
    pallas_call x2 -> x1, Pallas kernels: 74.9 us -> 201 us  [moe_layer(): pl.pallas_call(functools.partial(moe_kernel, num_experts), in_specs=[vmem...]
    all_gather x2 -> x0, waiting for transfers between devices: 42 us -> none  [local_step(): lax.all_gather(send[c * chunk:(c + 1) * chunk], 'ep', axis=0, tiled=True)]
    unnamed x34 -> x23, local copies, waits for them, and re-layouts: 29.7 us -> 11.9 us
  transfers between devices with their start and end apart: 4 -> 0, of which waited for: 4 -> 0; matrix products, arithmetic and copies ran while one was open for 4% -> 0% of each run, Pallas kernels for 13% -> 0%
where the time goes in v2:
time: 320 us; the launch traced here: 319 us
  Pallas kernels  298 us (93%)
  local copies, waits for them, and re-layouts  19.2 us (6%)
    pallas_call x1, Pallas kernels, moe_layer(): pl.pallas_call(functools.partial(moe_kernel, num_experts), in_specs=[vmem...  201 us
    pallas_call x1, Pallas kernels, attend(): pl.pallas_call(functools.partial(attend_kernel, batch, ahead, kv_heads, n...  60.4 us
    pallas_call x1, Pallas kernels, qkv_project(): pl.pallas_call(functools.partial(qkv_kernel, head_dim, q_steps, kv_steps)...  22 us
    pallas_call x1, Pallas kernels, post_attention(): pl.pallas_call(functools.partial(post_kernel, num_experts, steps), grid=(...  15 us
    unnamed x23, local copies, waits for them, and re-layouts  11.9 us

profile of v2, /device:TPU:0, one launch (start us, length us, event | category | flops | bytes accessed | tf_op | source)
XLA Modules:
  0.0 319.2 jit_solution(13541176214106224489)
XLA Ops:
  0.6 0.7 convert_element_type.5
  1.3 0.7 broadcast_in_dim.35.bk_ref
  2.0 0.7 broadcast_in_dim.36.bv_ref
  2.7 0.7 broadcast_in_dim.32.gain_ref
  3.4 0.7 broadcast_in_dim.33.bias_ref
  4.1 0.7 broadcast_in_dim.34.bq_ref
  4.8 0.7 broadcast_in_dim.37.bo_ref
  5.5 0.7 broadcast_in_dim.38.gain_ref
  6.2 0.7 broadcast_in_dim.39.bias_ref
  7.0 0.8 copy.28.one_ref
  7.7 0.8 copy.29.two_ref
  8.5 0.8 copy.27
  9.3 0.3 fusion
  9.6 0.1 pad_maximum_fusion
  9.7 1.4 copy.26
  11.1 0.2 pad.8.wr_ref
  11.3 0.0 copy-start
  11.3 3.4 %copy-done = bf16[4096,1024]{1,0:T(8,128)(2,1)S(1)} copy-done((bf16[4096,1024]{1,0:T(8,128)(2,1)S(1)}, bf16[4096,1024]{1,0:T(8,128)(2,1)}, u32[]{:S(2)}) %copy-start) | copy-done | bytes 8388632
  14.7 0.0 copy-start.1
  14.7 1.2 copy-done.1
  15.9 0.0 copy-start.5
  15.9 22.0 %shard_map.238 = (bf16[128,4096]{1,0:T(8,128)(2,1)S(1)}, bf16[128,1024]{1,0:T(8,128)(2,1)S(1)}, bf16[128,1024]{1,0:T(8,128)(2,1)S(1)}) custom-call(bf16[128,4096]{1,0:T(8,128)(2,1)S(1)} %copy-done.1, bf16[1,4096]{1,0:T(2,128)(2,1)S(1)} %broadcast_in_dim.32.gain_ref, bf16[1,4096]{1,0:T(2,128)(2,1)S(1)} %broadcast_in_dim.33.bias_ref, ...), custom_call_target="tpu_custom_call" | custom-call | flops 6442450944 | bytes 50331648 | tf_op jit(solution)/shard_map/pallas_call | solution.py:80
  37.9 0.2 copy.30
  38.2 0.0 copy-start.3
  38.3 0.0 copy-start.4
  38.3 0.0 copy-done.5
  38.3 0.0 copy-start.2
  38.3 60.4 %shard_map.239 = bf16[128,32,128]{2,1,0:T(8,128)(2,1)S(1)} custom-call(s32[128]{0:T(128)S(1)} %copy-done.5, bf16[128,32,128]{2,1,0:T(8,128)(2,1)S(1)} %bitcast.15, bf16[128,8,128]{2,1,0:T(8,128)(2,1)S(1)} %bitcast.17, bf16[128,8,128]{2,1,0:T(8,128)(2,1)S(1)} %bitcast.19, bf16[128,128,8,128]{3,2,1,0:T(8,128)(2,1)} %k_hbm.1, bf16[128,128,8,128]{3,2,1,0:T(8,128)(2,1)} %v_hbm.1), custom_call_target="tpu_custom_call" | custom-call | flops 2147483648 | bytes 67108864 | tf_op jit(solution)/shard_map/pallas_call | solution.py:160
  98.7 0.0 copy-done.3
  98.7 0.0 copy-done.4
  98.7 0.5 copy.35
  99.2 0.0 copy-done.2
  99.2 15.0 %shard_map.240 = (bf16[128,4096]{1,0:T(8,128)(2,1)S(1)}, bf16[128,4224]{1,0:T(8,128)(2,1)S(1)}) custom-call(bf16[128,4096]{1,0:T(8,128)(2,1)S(1)} %bitcast.14, bf16[4096,4096]{1,0:T(8,128)(2,1)} %wo_ref.1, bf16[1,4096]{1,0:T(2,128)(2,1)S(1)} %broadcast_in_dim.37.bo_ref, bf16[128,4096]{1,0:T(8,128)(2,1)S(1)} %copy-done.2, ...), custom_call_target="tpu_custom_call" | custom-call | flops 4294967296 | bytes 33554432 | tf_op jit(solution)/shard_map/pallas_call | solution.py:223
  114.2 0.0 copy-start.6
  114.2 1.0 copy-done.6
  115.2 0.0 copy-start.7
  115.2 1.0 copy-done.7
  116.2 200.8 %shard_map.241 = (bf16[128,4096]{1,0:T(8,128)(2,1)}, bf16[16,128,4224]{2,1,0:T(8,128)(2,1)}) custom-call(bf16[128,4224]{1,0:T(8,128)(2,1)} %copy-done.6, bf16[128,4096]{1,0:T(8,128)(2,1)} %copy-done.7, bf16[1,960,4096]{2,1,0:T(8,128)(2,1)} %bitcast.26, bf16[1,960,4096]{2,1,0:T(8,128)(2,1)} %bitcast.27, bf16[1,960,4096]{2,1,0:T(8,128)(2,1)} %wd_hbm.1), custom_call_target="tpu_custom_call" | custom-call | flops 48318382080 | bytes 23592960 | tf_op jit(solution)/shard_map/pallas_call | solution.py:489
  316.9 2.3 copy.37
  (4 shorter events, 0.1 us)
Async XLA Ops:
  11.3 3.4 %copy-start = (bf16[4096,1024]{1,0:T(8,128)(2,1)S(1)}, bf16[4096,1024]{1,0:T(8,128)(2,1)}, u32[]{:S(2)}) copy-start(bf16[4096,1024]{1,0:T(8,128)(2,1)} %wk_ref.1) | copy-start | bytes 25165828
  14.7 1.2 copy-start.1
  15.9 22.4 %copy-start.5 = (s32[128]{0:T(128)S(1)}, s32[128]{0:T(128)}, u32[]{:S(2)}) copy-start(s32[128]{0:T(128)} %pos_ref.1) | copy-start | bytes 1540
  38.2 60.5 %copy-start.3 = (bf16[16,8,8,128]{3,2,1,0:T(8,128)(2,1)}, bf16[16,8,8,128]{3,2,1,0:T(8,128)(2,1)S(1)}, u32[]{:S(2)}) copy-start(bf16[16,8,8,128]{3,2,1,0:T(8,128)(2,1)S(1)} %copy.31) | copy-start | bytes 786436
  38.3 60.4 %copy-start.4 = (bf16[16,8,8,128]{3,2,1,0:T(8,128)(2,1)}, bf16[16,8,8,128]{3,2,1,0:T(8,128)(2,1)S(1)}, u32[]{:S(2)}) copy-start(bf16[16,8,8,128]{3,2,1,0:T(8,128)(2,1)S(1)} %copy.32) | copy-start | bytes 786436
  38.3 60.9 %copy-start.2 = (bf16[128,4096]{1,0:T(8,128)(2,1)S(1)}, bf16[128,4096]{1,0:T(8,128)(2,1)}, u32[]{:S(2)}) copy-start(bf16[128,4096]{1,0:T(8,128)(2,1)} %tok_ref.3) | copy-start | bytes 3145732
  114.2 1.0 copy-start.6
  115.2 1.0 copy-start.7

commit v3 on v2

--- a/solution.py
+++ b/solution.py
@@ -27,16 +27,16 @@
     return jnp.concatenate([cos_val, cos_val], axis=-1), jnp.concatenate([-sin_val, sin_val], axis=-1)
 
 
-def qkv_kernel(head_dim, q_steps, kv_steps, tok_ref, gain_ref, bias_ref, cos_ref, sin_ref, wq_ref, wk_ref, wv_ref, bq_ref, bk_ref, bv_ref, q_ref, k_ref, v_ref, h_ref):
+def qkv_kernel(head_dim, q_steps, kv_steps, tok_ref, vec_ref, cos_ref, sin_ref, wq_ref, wk_ref, wv_ref, bq_ref, bkv_ref, q_ref, k_ref, v_ref, h_ref):
     step = pl.program_id(0)
 
     @pl.when(step == 0)
     def _():
         x = tok_ref[...].astype(jnp.float32)
-        h_ref[...] = layer_norm_rows(x, gain_ref[...].astype(jnp.float32), bias_ref[...].astype(jnp.float32)).astype(jnp.bfloat16)
-
-    def project(w_ref, b_ref):
-        return jnp.dot(h_ref[...], w_ref[...], preferred_element_type=jnp.float32) + b_ref[...].astype(jnp.float32)
+        h_ref[...] = layer_norm_rows(x, vec_ref[0:1, :], vec_ref[1:2, :]).astype(jnp.bfloat16)
+
+    def project(w_ref, b_row):
+        return jnp.dot(h_ref[...], w_ref[...], preferred_element_type=jnp.float32) + b_row
 
     def rotated(y, out_ref):
         for head in range(y.shape[1] // head_dim):
@@ -47,18 +47,18 @@
 
     @pl.when(step < q_steps)
     def _():
-        rotated(project(wq_ref, bq_ref), q_ref)
+        rotated(project(wq_ref, bq_ref[2:3, :]), q_ref)
 
     @pl.when((step >= q_steps) & (step < q_steps + kv_steps))
     def _():
-        rotated(project(wk_ref, bk_ref), k_ref)
+        rotated(project(wk_ref, bkv_ref[3:4, :]), k_ref)
 
     @pl.when(step >= q_steps + kv_steps)
     def _():
-        v_ref[...] = project(wv_ref, bv_ref).astype(jnp.bfloat16)
-
-
-def qkv_project(tokens, gain, bias, cos_tab, sin_tab, w_query, w_key, w_value, b_query, b_key, b_value, head_dim):
+        v_ref[...] = project(wv_ref, bkv_ref[3:4, :]).astype(jnp.bfloat16)
+
+
+def qkv_project(tokens, vecs, cos_tab, sin_tab, w_query, w_key, w_value, head_dim):
     rows, d_model = tokens.shape
     q_dim, kv_dim = w_query.shape[1], w_key.shape[1]
     block = 512
@@ -76,21 +76,23 @@
     def whole(arr):
         return pl.BlockSpec(arr.shape, lambda i: (0,) * arr.ndim)
 
-    gain, bias = gain[None, :], bias[None, :]
+    def kv_idx(i):
+        return (0, jnp.clip(i - q_steps, 0, 2 * kv_steps - 1))
+
     return pl.pallas_call(
         functools.partial(qkv_kernel, head_dim, q_steps, kv_steps),
         grid=(q_steps + 2 * kv_steps,),
         in_specs=[
-            whole(tokens), whole(gain), whole(bias), whole(cos_tab), whole(sin_tab),
+            whole(tokens), whole(vecs), whole(cos_tab), whole(sin_tab),
             pl.BlockSpec((d_model, block), q_idx), pl.BlockSpec((d_model, block), k_idx), pl.BlockSpec((d_model, block), v_idx),
-            pl.BlockSpec((1, block), q_idx), pl.BlockSpec((1, block), k_idx), pl.BlockSpec((1, block), v_idx),
+            pl.BlockSpec((vecs.shape[0], block), q_idx), pl.BlockSpec((vecs.shape[0], block), kv_idx),
         ],
         out_specs=[pl.BlockSpec((rows, block), q_idx), pl.BlockSpec((rows, block), k_idx), pl.BlockSpec((rows, block), v_idx)],
         out_shape=[jax.ShapeDtypeStruct((rows, q_dim), jnp.bfloat16), jax.ShapeDtypeStruct((rows, kv_dim), jnp.bfloat16), jax.ShapeDtypeStruct((rows, kv_dim), jnp.bfloat16)],
         scratch_shapes=[pltpu.VMEM((rows, d_model), jnp.bfloat16)],
-        compiler_params=pltpu.CompilerParams(dimension_semantics=("arbitrary",), vmem_limit_bytes=40 * MIB),
+        compiler_params=pltpu.CompilerParams(dimension_semantics=("arbitrary",), vmem_limit_bytes=62 * MIB),
         cost_estimate=pl.CostEstimate(flops=2 * rows * d_model * (q_dim + 2 * kv_dim), bytes_accessed=2 * d_model * (q_dim + 2 * kv_dim), transcendentals=0),
-    )(tokens, gain, bias, cos_tab, sin_tab, w_query, w_key, w_value, b_query[None, :], b_key[None, :], b_value[None, :])
+    )(tokens, vecs, cos_tab, sin_tab, w_query, w_key, w_value, vecs, vecs)
 
 
 def attend_kernel(batch, ahead, kv_heads, group_size, pos_ref, q_ref, kn_ref, vn_ref, k_hbm, v_hbm, out_ref, k_buf, v_buf, where_ref, k_sem, v_sem):
@@ -104,18 +106,28 @@
     head_ids = lax.broadcasted_iota(jnp.int32, (num_heads, cols), 0)
     where_ref[...] = jnp.where(col_ids % kv_heads == head_ids // group_size, col_ids // kv_heads, seq_len)
 
-    def copies(turn, lane):
+    half = seq_len // 2
+
+    def copies(turn, lane, part):
         tok = turn * batch + lane
         slot = lax.rem(turn, slots)
-        count = ((pos_ref[tok] + 7) // 8) * 8
-        k_copy = pltpu.make_async_copy(k_hbm.at[tok, pl.ds(0, count)], k_buf.at[slot, lane, pl.ds(0, count)], k_sem.at[slot])
-        v_copy = pltpu.make_async_copy(v_hbm.at[tok, pl.ds(0, count)], v_buf.at[slot, lane, pl.ds(0, count)], v_sem.at[slot])
+        rows = pl.ds(part * half, half)
+        k_copy = pltpu.make_async_copy(k_hbm.at[tok, rows], k_buf.at[slot, lane, rows], k_sem.at[slot])
+        v_copy = pltpu.make_async_copy(v_hbm.at[tok, rows], v_buf.at[slot, lane, rows], v_sem.at[slot])
         return k_copy, v_copy
 
+    def each(turn, act):
+        for lane in range(batch):
+            for copy in copies(turn, lane, 0):
+                act(copy)
+
+            @pl.when(pos_ref[turn * batch + lane] > half)
+            def _():
+                for copy in copies(turn, lane, 1):
+                    act(copy)
+
     def fetch(turn):
-        for lane in range(batch):
-            for copy in copies(turn, lane):
-                copy.start()
+        each(turn, lambda copy: copy.start())
 
     for turn in range(ahead):
         fetch(turn)
@@ -128,9 +140,7 @@
             fetch(turn + ahead)
 
         slot = lax.rem(turn, slots)
-        for lane in range(batch):
-            for copy in copies(turn, lane):
-                copy.wait()
+        each(turn, lambda copy: copy.wait())
         for lane in range(batch):
             tok = turn * batch + lane
             pos = pos_ref[tok]
@@ -168,24 +178,24 @@
     )(positions, q_heads, key_new, value_new, k_cache, v_cache)
 
 
-def post_kernel(num_experts, steps, attn_ref, wo_ref, bo_ref, tok_ref, gain_ref, bias_ref, wr_ref, one_ref, two_ref, elig_ref, x_ref, send_ref, acc_ref):
+def post_kernel(num_experts, steps, attn_ref, wo_ref, bo_ref, tok_ref, vec_ref, wr_ref, code_ref, x_ref, send_ref, acc_ref):
     step = pl.program_id(0)
     block = wo_ref.shape[1]
     cols = pl.ds(pl.multiple_of(step * block, block), block)
     mixed = jnp.dot(attn_ref[...], wo_ref[...], preferred_element_type=jnp.float32)
-    x_mid = (tok_ref[...].astype(jnp.float32) + mixed + bo_ref[...].astype(jnp.float32)).astype(jnp.bfloat16)
+    x_mid = (tok_ref[...].astype(jnp.float32) + mixed + bo_ref[4:5, :]).astype(jnp.bfloat16)
     x_ref[...] = x_mid
     acc_ref[:, cols] = x_mid
 
     @pl.when(step == steps - 1)
     def _():
-        h_two = layer_norm_rows(acc_ref[...].astype(jnp.float32), gain_ref[...].astype(jnp.float32), bias_ref[...].astype(jnp.float32)).astype(jnp.bfloat16)
-        logits = jnp.dot(h_two, wr_ref[...], preferred_element_type=jnp.float32)
-        rows, width = logits.shape
-        lanes = lax.broadcasted_iota(jnp.int32, (rows, width), 1)
-        hit_one = lanes == one_ref[...]
-        hit_two = lanes == two_ref[...]
-        keep_one = elig_ref[...] == 1
+        h_two = layer_norm_rows(acc_ref[...].astype(jnp.float32), vec_ref[5:6, :], vec_ref[6:7, :]).astype(jnp.bfloat16)
+        code = code_ref[...]
+        routes = jnp.concatenate([wr_ref[...], jnp.zeros((code.shape[1] - num_experts, wr_ref.shape[1]), jnp.bfloat16)], axis=0)
+        logits = lax.dot_general(h_two, routes, (((1,), (1,)), ((), ())), preferred_element_type=jnp.float32)
+        hit_one = (code & 2) == 2
+        hit_two = (code & 4) == 4
+        keep_one = (code & 1) == 1
         keep_two = keep_one & jnp.logical_not(hit_one)
 
         def gate(keep, hit):
@@ -203,16 +213,16 @@
         send_ref[:, d_model:] = packed.astype(jnp.bfloat16)
 
 
-def post_attention(attn, w_out, b_out, tokens, gain, bias, w_router, expert_one, expert_two, eligible):
+def post_attention(attn, w_out, tokens, vecs, w_router, expert_one, expert_two, eligible):
     rows, d_model = tokens.shape
     num_experts = w_router.shape[1]
     width = 128
     block = 512
     steps = d_model // block
-    w_router = jnp.pad(w_router, ((0, 0), (0, width - num_experts)))
-    eligible = jnp.pad(eligible, ((0, 0), (0, width - num_experts)))
-    one, two = expert_one[:, None], expert_two[:, None]
-    gain, bias = gain[None, :], bias[None, :]
+    routes = jnp.swapaxes(w_router, 0, 1)
+    ids = jnp.arange(num_experts, dtype=jnp.int32)[None, :]
+    code = (eligible == 1).astype(jnp.int32) + 2 * (expert_one[:, None] == ids) + 4 * (expert_two[:, None] == ids)
+    code = jnp.pad(code, ((0, 0), (0, width - num_experts)))
 
     def whole(arr):
         return pl.BlockSpec(arr.shape, lambda i: (0,) * arr.ndim)
@@ -224,15 +234,15 @@
         functools.partial(post_kernel, num_experts, steps),
         grid=(steps,),
         in_specs=[
-            whole(attn), pl.BlockSpec((attn.shape[1], block), col), pl.BlockSpec((1, block), col), pl.BlockSpec((rows, block), col),
-            whole(gain), whole(bias), whole(w_router), whole(one), whole(two), whole(eligible),
+            whole(attn), pl.BlockSpec((attn.shape[1], block), col), pl.BlockSpec((vecs.shape[0], block), col), pl.BlockSpec((rows, block), col),
+            whole(vecs), whole(routes), whole(code),
         ],
         out_specs=[pl.BlockSpec((rows, block), col), pl.BlockSpec((rows, d_model + width), lambda i: (0, 0))],
         out_shape=[jax.ShapeDtypeStruct((rows, d_model), jnp.bfloat16), jax.ShapeDtypeStruct((rows, d_model + width), jnp.bfloat16)],
         scratch_shapes=[pltpu.VMEM((rows, d_model), jnp.bfloat16)],
-        compiler_params=pltpu.CompilerParams(dimension_semantics=("arbitrary",), vmem_limit_bytes=48 * MIB),
+        compiler_params=pltpu.CompilerParams(dimension_semantics=("arbitrary",), vmem_limit_bytes=62 * MIB),
         cost_estimate=pl.CostEstimate(flops=2 * rows * d_model * d_model, bytes_accessed=2 * d_model * d_model, transcendentals=0),
-    )(attn, w_out, b_out[None, :], tokens, gain, bias, w_router, one, two, eligible)
+    )(attn, w_out, vecs, tokens, vecs, routes, code)
 
 
 STEP_ROWS = 16
@@ -272,54 +282,64 @@
         pl.semaphore_signal(barrier, inc=1, device_id=(peer,), device_id_type=logical)
     pl.semaphore_wait(barrier, DIMS + 1)
 
-    def piece(owner, part, mine):
+    def piece(owner, half, part, mine):
         cols = pl.ds(part * third, third)
-        src = h_ref.at[:, cols] if mine else all_ref.at[owner, :, cols]
-        return src, all_ref.at[owner, :, cols]
-
-    def spread(owner, part, slot, peer, mine):
-        src, dst = piece(owner, part, mine)
-        return pltpu.make_async_remote_copy(src, dst, gs_sem.at[part, slot], gr_sem.at[part, slot], device_id=(peer,), device_id_type=logical)
-
-    def share(owner, part, slot, mine):
-        src, dst = piece(owner, part, mine)
-        return pltpu.make_async_remote_copy(src, dst, ms_sem.at[part, slot], mr_sem.at[part, slot], device_id=(mate,), device_id_type=logical)
-
-    started = []
-    for part in range(3):
-        copy = share(me, part, 0, True)
-        copy.start()
-        started.append(copy)
-    held = [[chip] for _ in range(3)]
-    base = 0
-    for step in range(DIMS):
-        wave = []
-        for part in range(3):
-            dim = (part + step) % 3
-            for n, who in enumerate(held[part]):
-                copy = spread(device_of(who), part, base + n, peers[dim], n == 0)
-                copy.start()
-                wave.append(copy)
-                started.append(copy)
-        for part in range(3):
-            dim = (part + step) % 3
-            count = len(held[part])
-            fresh = [across(who, dim) for who in held[part]]
-            for n, who in enumerate(fresh):
-                wave[part * count + n].wait_recv()
-                copy = share(device_of(who), part, 1 + base + n, False)
-                copy.start()
-                started.append(copy)
-            held[part] = held[part] + fresh
-        base += 1 << step
+        some = pl.ds(half * (rows // 2), rows // 2)
+        src = h_ref.at[some, cols] if mine else all_ref.at[owner, some, cols]
+        return src, all_ref.at[owner, some, cols]
+
+    def spread(owner, half, part, slot, peer, mine):
+        src, dst = piece(owner, half, part, mine)
+        return pltpu.make_async_remote_copy(src, dst, gs_sem.at[half, part, slot], gr_sem.at[half, part, slot], device_id=(peer,), device_id_type=logical)
+
+    def share(owner, half, part, slot, mine):
+        src, dst = piece(owner, half, part, mine)
+        return pltpu.make_async_remote_copy(src, dst, ms_sem.at[half, part, slot], mr_sem.at[half, part, slot], device_id=(mate,), device_id_type=logical)
+
+    def held(part, step):
+        whos = [chip]
+        for k in range(step):
+            whos = whos + [across(who, (part + k) % 3) for who in whos]
+        return whos
+
+    def wave(half, step):
+        base = (1 << step) - 1
+        return [spread(device_of(who), half, part, base + n, peers[(part + step) % 3], n == 0) for part in range(3) for n, who in enumerate(held(part, step))]
+
+    def shares(half, step):
+        base = 1 << step
+        return [share(device_of(across(who, (part + step) % 3)), half, part, base + n, False) for part in range(3) for n, who in enumerate(held(part, step))]
+
+    def own_shares(half):
+        return [share(me, half, part, 0, True) for part in range(3)]
+
+    def send(half, step):
+        for copy in wave(half, step):
+            copy.start()
+
+    def take(half, step):
+        for landed, onward in zip(wave(half, step), shares(half, step)):
+            landed.wait_recv()
+            onward.start()
+
+    def shared(half):
+        for copy in own_shares(half) + shares(half, 0) + shares(half, 1) + shares(half, 2):
+            copy.wait_recv()
+
+    for half in range(2):
+        for copy in own_shares(half):
+            copy.start()
+    send(0, 0)
+    send(1, 0)
+    for step in range(2):
+        for half in range(2):
+            take(half, step)
+            send(half, step + 1)
+    take(0, 2)
     for copy in weights:
         copy.wait()
     own.wait()
-    for part in range(3):
-        for slot in range(8):
-            share(me, part, slot, True).wait_recv()
-    for copy in started:
-        copy.wait_send()
+    shared(0)
 
     spans = []
     at = 0
@@ -441,6 +461,14 @@
     x_copy(0).start()
 
     def turn(i, carry):
+        @pl.when(i == 2)
+        def _():
+            take(1, 2)
+
+        @pl.when(i == chunks // 2 - 1)
+        def _():
+            shared(1)
+
         @pl.when(i < chunks)
         def _():
             experts(i)
@@ -464,6 +492,9 @@
         return carry
 
     lax.fori_loop(0, chunks + 4, turn, 0)
+    for half in range(2):
+        for copy in own_shares(half) + shares(half, 0) + shares(half, 1) + shares(half, 2) + wave(half, 0) + wave(half, 1) + wave(half, 2):
+            copy.wait_send()
     for c in (chunks - 2, chunks - 1):
         mate_copy(c).wait_send()
         for level in range(3):
@@ -497,7 +528,7 @@
             pltpu.VMEM((2, chips, 2, STEP_ROWS, d_model), f32),
             pltpu.VMEM((2, chips, STEP_ROWS, d_model), f32),
             level_bufs(), level_bufs(), level_bufs(),
-            dma((3,)), dma, dma, dma((3, 7)), dma((3, 7)), dma((3, 8)), dma((3, 8)),
+            dma((3,)), dma, dma, dma((2, 3, 7)), dma((2, 3, 7)), dma((2, 3, 8)), dma((2, 3, 8)),
             dma((2,)), dma((2,)), regular, dma((9, 2)), dma((9, 2)), regular((9,)),
         ],
         compiler_params=pltpu.CompilerParams(collective_id=0, has_side_effects=True, vmem_limit_bytes=67043328),
@@ -512,12 +543,15 @@
         _, seq_len, kv_heads, head_dim = k_cache.shape
         num_heads = w_query.shape[1] // head_dim
         num_experts = w_router.shape[1]
+        kv_dim = b_key.shape[0]
+        kv_bias = jnp.concatenate([b_key, b_value, jnp.zeros((d_model - 2 * kv_dim,), b_key.dtype)])
+        vecs = jnp.stack([ln1_gain, ln1_bias, b_query, kv_bias, b_out, ln2_gain, ln2_bias, ln2_bias]).astype(jnp.float32)
         cos_tab, sin_tab = rope_tables(positions, head_dim)
-        q_flat, k_flat, v_flat = qkv_project(tokens, ln1_gain, ln1_bias, cos_tab, sin_tab, w_query, w_key, w_value, b_query, b_key, b_value, head_dim)
+        q_flat, k_flat, v_flat = qkv_project(tokens, vecs, cos_tab, sin_tab, w_query, w_key, w_value, head_dim)
         key_new = k_flat.reshape(rows, kv_heads, head_dim)
         value_new = v_flat.reshape(rows, kv_heads, head_dim)
         attn = attend(positions, q_flat.reshape(rows, num_heads, head_dim), key_new, value_new, k_cache, v_cache)
-        x_mid, send = post_attention(attn.reshape(rows, num_heads * head_dim), w_out, b_out, tokens, ln2_gain, ln2_bias, w_router, expert_one, expert_two, eligible)
+        x_mid, send = post_attention(attn.reshape(rows, num_heads * head_dim), w_out, tokens, vecs, w_router, expert_one, expert_two, eligible)
         tokens_out = moe_layer(send, x_mid, w_gate, w_up, w_down, num_experts)
         return tokens_out, key_new, value_new
 

time: 320 us -> 302 us (0.944)
  Pallas kernels: 298 us -> 284 us
  local copies, waits for them, and re-layouts: 19.2 us -> 12.4 us
  other arithmetic: 1.08 us -> 4.56 us
    pallas_call x1, Pallas kernels: 201 us -> 181 us  [moe_layer(): pl.pallas_call(functools.partial(moe_kernel, num_experts), in_specs=[vmem...]
    broadcast_in_dim x10 -> x1, local copies, waits for them, and re-layouts: 7.16 us -> 0.01 us  [local_step(): jnp.zeros((d_model - 2 * kv_dim,), b_key.dtype)]
    unnamed x23 -> x11, local copies, waits for them, and re-layouts: 11.9 us -> 7.24 us
    another operation x0 -> x8, local copies, waits for them, and re-layouts: none -> 4.47 us  [local_step(): jnp.stack([ln1_gain, ln1_bias, b_query, kv_bias, b_out, ln2_gain, ln2_bia...]
    pallas_call x1, Pallas kernels: 22 us -> 26.3 us  [qkv_project(): pl.pallas_call(functools.partial(qkv_kernel, head_dim, q_steps, kv_steps)...]
where the time goes in v3:
time: 302 us
  Pallas kernels  284 us (94%)
  local copies, waits for them, and re-layouts  12.4 us (4%)
  other arithmetic  4.56 us (2%)
    pallas_call x1, Pallas kernels, moe_layer(): pl.pallas_call(functools.partial(moe_kernel, num_experts), in_specs=[vmem...  181 us
    pallas_call x1, Pallas kernels, attend(): pl.pallas_call(functools.partial(attend_kernel, batch, ahead, kv_heads, n...  59.9 us
    pallas_call x1, Pallas kernels, qkv_project(): pl.pallas_call(functools.partial(qkv_kernel, head_dim, q_steps, kv_steps)...  26.3 us
    pallas_call x1, Pallas kernels, post_attention(): pl.pallas_call(functools.partial(post_kernel, num_experts, steps), grid=(...  17.1 us
    unnamed x11, local copies, waits for them, and re-layouts  7.24 us

profile of v3, /device:TPU:0, one launch (start us, length us, event | category | flops | bytes accessed | tf_op | source)
XLA Modules:
  0.0 301.6 jit_solution(14836653716573313300)
XLA Ops:
  0.6 0.7 convert_element_type.12
  1.3 0.7 pad_maximum_fusion.2
  2.0 0.7 compare_convert_fusion
  2.7 0.7 stack.25
  3.4 0.7 stack.26
  4.2 0.7 stack.27
  4.9 0.7 stack.29
  5.6 0.7 stack.30
  6.3 0.7 stack.31
  7.0 0.2 stack.32
  7.2 0.1 copy.28
  7.3 0.8 select_add_fusion
  8.1 0.6 pad.4.code_ref
  8.7 0.7 convert_element_type.11.vec_ref.bq_ref.bkv_ref.bo_ref
  9.4 0.3 fusion
  9.7 0.7 pad_maximum_fusion
  10.4 0.0 copy-start.2
  10.4 26.3 %shard_map.238 = (bf16[128,4096]{1,0:T(8,128)(2,1)}, bf16[128,1024]{1,0:T(8,128)(2,1)}, bf16[128,1024]{1,0:T(8,128)(2,1)}) custom-call(bf16[128,4096]{1,0:T(8,128)(2,1)} %tok_ref.3, f32[8,4096]{1,0:T(8,128)} %convert_element_type.11.vec_ref.bq_ref.bkv_ref.bo_ref, f32[128,128]{1,0:T(8,128)} %get-tuple-element.18.cos_ref, ...), custom_call_target="tpu_custom_call" | custom-call | flops 6442450944 | bytes 50331648 | tf_op jit(solution)/shard_map/pallas_call | solution.py:82
  36.7 1.4 copy.29
  38.2 1.0 copy.30
  39.2 0.0 copy-start
  39.2 1.1 copy.31
  40.3 0.0 copy-start.1
  40.3 0.0 copy-done.2
  40.3 59.9 %shard_map.239 = bf16[128,32,128]{2,1,0:T(8,128)(2,1)S(1)} custom-call(s32[128]{0:T(128)S(1)} %copy-done.2, bf16[128,32,128]{2,1,0:T(8,128)(2,1)S(1)} %bitcast.13, bf16[128,8,128]{2,1,0:T(8,128)(2,1)S(1)} %bitcast.15, bf16[128,8,128]{2,1,0:T(8,128)(2,1)S(1)} %bitcast.17, bf16[128,128,8,128]{3,2,1,0:T(8,128)(2,1)} %k_hbm.1, bf16[128,128,8,128]{3,2,1,0:T(8,128)(2,1)} %v_hbm.1), custom_call_target="tpu_custom_call" | custom-call | flops 2147483648 | bytes 67108864 | tf_op jit(solution)/shard_map/pallas_call | solution.py:170
  100.2 0.0 copy-done
  100.2 0.0 copy-done.1
  100.2 1.4 copy.34
  101.6 17.1 %shard_map.240 = (bf16[128,4096]{1,0:T(8,128)(2,1)}, bf16[128,4224]{1,0:T(8,128)(2,1)}) custom-call(bf16[128,4096]{1,0:T(8,128)(2,1)} %bitcast.19, bf16[4096,4096]{1,0:T(8,128)(2,1)} %wo_ref.1, f32[8,4096]{1,0:T(8,128)} %convert_element_type.11.vec_ref.bq_ref.bkv_ref.bo_ref, bf16[128,4096]{1,0:T(8,128)(2,1)} %tok_ref.3, ...), custom_call_target="tpu_custom_call" | custom-call | flops 4294967296 | bytes 33554432 | tf_op jit(solution)/shard_map/pallas_call | solution.py:233
  118.7 180.6 %shard_map.241 = (bf16[128,4096]{1,0:T(8,128)(2,1)}, bf16[16,128,4224]{2,1,0:T(8,128)(2,1)}) custom-call(bf16[128,4224]{1,0:T(8,128)(2,1)} %get-tuple-element.12.h_ref, bf16[128,4096]{1,0:T(8,128)(2,1)} %get-tuple-element.13.xm_ref, bf16[1,960,4096]{2,1,0:T(8,128)(2,1)} %bitcast.24, bf16[1,960,4096]{2,1,0:T(8,128)(2,1)} %bitcast.25, bf16[1,960,4096]{2,1,0:T(8,128)(2,1)} %wd_hbm.1), custom_call_target="tpu_custom_call" | custom-call | flops 48318382080 | bytes 23592960 | tf_op jit(solution)/shard_map/pallas_call | solution.py:520
  299.3 2.3 copy.36
  (3 shorter events, 0.0 us)
Async XLA Ops:
  10.4 29.9 %copy-start.2 = (s32[128]{0:T(128)S(1)}, s32[128]{0:T(128)}, u32[]{:S(2)}) copy-start(s32[128]{0:T(128)} %pos_ref.1) | copy-start | bytes 1540
  39.2 61.0 %copy-start = (bf16[16,8,8,128]{3,2,1,0:T(8,128)(2,1)}, bf16[16,8,8,128]{3,2,1,0:T(8,128)(2,1)S(1)}, u32[]{:S(2)}) copy-start(bf16[16,8,8,128]{3,2,1,0:T(8,128)(2,1)S(1)} %copy.30) | copy-start | bytes 786436
  40.3 59.9 %copy-start.1 = (bf16[16,8,8,128]{3,2,1,0:T(8,128)(2,1)}, bf16[16,8,8,128]{3,2,1,0:T(8,128)(2,1)S(1)}, u32[]{:S(2)}) copy-start(bf16[16,8,8,128]{3,2,1,0:T(8,128)(2,1)S(1)} %copy.31) | copy-start | bytes 786436
